TPU v7x, 256 devices: a whole 4x4x8 slice. The times are simulated.
256 devices in a mesh: space: 32 (over z, y_hi, core), tm: 8 (over x, y_lo).
Axes of the slice: x: 4, y: 4 (y_hi: 2, y_lo: 2; y = y_hi * 2 + y_lo), z: 8, core: 2. Of those that a mesh axis runs over, the one named last changes fastest.
Arguments:
- solutions: bfloat16 [8, 12, 16384, 128], P('tm', None, 'space'), may hold values from -6 to 6
- noise: int32 [8, 64, 12, 16384], P('tm', None, None, 'space'), may hold values from 0 to 3
- momenta: int32 [27, 3], replicated, may hold values from -2 to 2
- pairs: int32 [64, 2], P('tm'), may hold values from 0 to 7
Outputs:
- mesons: float32 [8, 2, 27, 64, 64], P('tm', None, None, 'space')
- correlators: float32 [64, 2, 27], P('tm')
All inputs are finite; a program needn't handle non-finite values.
Results may differ from a plain program's by a relative error of at most 0.002.
Values sent between devices are 32-bit elements; how exact they have to be, the bound alone decides.
No kernel may reach another device: no remote copies, remote signals or barrier semaphores. Data moves between devices by JAX's collectives and lax.ppermute only.
A program may use at most 64 MiB of HBM per device.

v0:
```python
import math

import jax
import jax.numpy as jnp
from jax import lax
from jax.sharding import PartitionSpec as P

EXTENT = 48


def in_blocks(array, dim, length):
    before, after = (array.shape[:dim], array.shape[dim + 1 :])
    return jnp.moveaxis(array.reshape(*before, length, -1, *after), dim, 0)


def summed_on_arrival(array, axis, dim):
    pieces = in_blocks(array, dim, lax.axis_size(axis))
    arrived = lax.all_to_all(pieces, axis, split_axis=0, concat_axis=0, tiled=True)
    return arrived.sum(axis=0)


def copy_for_each(array, axis):
    copies = jnp.broadcast_to(array, (lax.axis_size(axis), *array.shape))
    return lax.all_to_all(copies, axis, split_axis=0, concat_axis=0, tiled=True)


def laid_out(pieces, dim):
    pieces = jnp.moveaxis(pieces, 0, dim)
    dims = pieces.shape
    return pieces.reshape(*dims[:dim], dims[dim] * dims[dim + 1], *dims[dim + 2 :])


def gathered_copies(array, axis, dim):
    pieces = copy_for_each(array, axis)
    return laid_out(pieces, dim)


def over_copies(array, axis):
    return copy_for_each(array, axis).sum(axis=0)


def phase_weights(noise_block, momenta, coords):
    qdotx = (
        momenta[:, 0:1] * coords[0][None, :]
        + momenta[:, 1:2] * coords[1][None, :]
        + momenta[:, 2:3] * coords[2][None, :]
    )
    base_index = qdotx % EXTENT
    angle = base_index.astype(jnp.float32) * jnp.float32(2.0 * math.pi / EXTENT)
    base_re = jnp.cos(angle).astype(jnp.bfloat16)[:, None, None, :]
    base_im = (-jnp.sin(angle)).astype(jnp.bfloat16)[:, None, None, :]
    turns = (noise_block % 4)[None, :, :, :]
    weight_re = jnp.where(
        turns == 0,
        base_re,
        jnp.where(turns == 1, base_im, jnp.where(turns == 2, -base_re, -base_im)),
    )
    weight_im = jnp.where(
        turns == 0,
        base_im,
        jnp.where(turns == 1, -base_re, jnp.where(turns == 2, -base_im, base_re)),
    )
    rows = momenta.shape[0] * noise_block.shape[0]
    cols = noise_block.shape[1] * noise_block.shape[2]
    return (weight_re.reshape(rows, cols), weight_im.reshape(rows, cols))


def partial_field(vectors, sources, momenta, offset):
    spincol, sites, width = vectors.shape
    nvec = width // 2
    moms = momenta.shape[0]
    block = min(128, sites)
    nblocks = sites // block

    def one_block(step, total):
        first = (step * block).astype(jnp.int32)
        noise_block = lax.dynamic_slice_in_dim(sources, first, block, 2)
        vec_block = lax.dynamic_slice_in_dim(vectors, first, block, 1)
        glob = offset + first + jnp.arange(block, dtype=jnp.int32)
        coords = (glob % EXTENT, glob // EXTENT % EXTENT, glob // (EXTENT * EXTENT))
        weight_re, weight_im = phase_weights(noise_block, momenta, coords)
        stacked = vec_block.reshape(spincol * block, width)
        left = jnp.dot(weight_re, stacked, preferred_element_type=jnp.float32)
        right = jnp.dot(weight_im, stacked, preferred_element_type=jnp.float32)
        real_part = left[:, :nvec] - right[:, nvec:]
        imag_part = left[:, nvec:] + right[:, :nvec]
        return total + jnp.stack([real_part, imag_part], 0)

    start = jnp.zeros((2, moms * nvec, nvec), jnp.float32)
    total = lax.fori_loop(0, nblocks, one_block, start)
    return total.reshape(2, moms, nvec, nvec)


def pair_traces(fields, pairs):
    nslices = fields.shape[0]
    slots = jnp.arange(nslices, dtype=jnp.int32)
    pick_sink = (pairs[:, 1][:, None] == slots[None, :]).astype(jnp.float32)
    pick_source = (pairs[:, 0][:, None] == slots[None, :]).astype(jnp.float32)
    sink = jnp.einsum("kt,tcpij->kcpij", pick_sink, fields, precision=lax.Precision.HIGHEST)
    source = jnp.einsum("kt,tcpij->kcpij", pick_source, fields, precision=lax.Precision.HIGHEST)
    real_part = jnp.sum(sink[:, 0] * source[:, 0] + sink[:, 1] * source[:, 1], axis=(2, 3))
    imag_part = jnp.sum(sink[:, 1] * source[:, 0] - sink[:, 0] * source[:, 1], axis=(2, 3))
    return jnp.stack([real_part, imag_part], 1)


def local(solutions, noise, momenta, pairs):
    slice_count, spincol, sites_local, width = solutions.shape
    nvec = width // 2
    nspace = lax.axis_size("space")
    scale = 1.0 / math.sqrt(spincol * sites_local * nspace)
    offset = lax.axis_index("space") * sites_local
    terms = jnp.stack([partial_field(solutions[0], noise[0], momenta, offset) * scale], 0)
    mesons = summed_on_arrival(terms, "space", 3)
    every_slice = gathered_copies(mesons, "tm", 0)
    partial_traces = pair_traces(every_slice, pairs)
    correlators = over_copies(partial_traces, "space") / nvec
    return (mesons, correlators)


def solution(mesh):
    in_specs = (P("tm", None, "space", None), P("tm", None, None, "space"), P(), P("tm", None))
    out_specs = (P("tm", None, None, "space", None), P("tm", None, None))
    return jax.shard_map(local, mesh=mesh, in_specs=in_specs, out_specs=out_specs, check_vma=False)
```

profile of v0, /device:TPU:1, one launch (start us, length us, event | category | flops | bytes accessed | tf_op | source)
XLA Modules:
  0.0 147.4 jit_solution(9370178631061712609)
XLA Ops:
  0.7 3.8 %copy.60 = s32[1,64,12,512]{3,2,1,0:T(8,128)} copy(s32[1,64,12,512]{3,1,2,0:T(8,128)} %param.7) | data formatting | bytes 3145728 | tf_op args[1]
  4.4 64.5 %while.17 = (s32[]{:T(128)}, f32[2,1728,64]{2,1,0:T(8,128)S(1)}, s32[64,12,512]{2,1,0:T(8,128)}, s32[27,3]{0,1:T(4,128)S(1)}, s32[]{:T(128)}, /*index=5*/bf16[12...) while((s32[]{:T(128)}, f32[2,1728,64]{2,1,0:T(8,128)S(1)}, ...), condition=%wide.region_1.2_spmd.clone, body=%wide.region_0.1_spmd.clone.sunk | while | flops 1377275648 | bytes 30928840 | solution.py:90
  4.8 1.4 broadcast_compare_fusion.4
  6.3 5.9 %select_select_fusion.3 = (bf16[27,64,12,128]{3,2,1,0:T(8,128)(2,1)}, bf16[27,64,12,128]{3,2,1,0:T(8,128)(2,1)S(1)}) fusion(pred[64,12,128]{2,1,0:T(8,128)(4,1)S(1)} %get-tuple-element.305, pred[64,12,128]{2,1,0:T(8,128)(4,1)S(1)} %get-tuple-element.306, pred[64,12,128]{2,1,0:T(8,128)(4,1)S(1)} %get-tuple-element.307, ...), kind=kLoop, calls=%fused_computation.1.clone.1 | loop fusion | flops 15925248 | bytes 10939392 | tf_op jit(solution)/shard_map/while/body/eval_jaxpr/jit(_where)/select_n | solution.py:53
  13.2 4.6 %fusion.46 = f32[1728,128]{1,0:T(8,128)S(1)} fusion(bf16[1536,128]{1,0:T(8,128)(2,1)S(1)} %bitcast.77, bf16[216,8,12,128]{3,2,1,0:T(8,128)(2,1)} %bitcast.75), kind=kOutput, calls=%fused_computation.5.clone.1 | convolution fusion | flops 679477248 | bytes 6586368 | tf_op jit(solution)/shard_map/while/body/eval_jaxpr/dot_general | solution.py:83
  17.8 1.6 %fusion.45 = f32[1728,128]{1,0:T(8,128)S(1)} fusion(bf16[1536,128]{1,0:T(8,128)(2,1)S(1)} %bitcast.78, bf16[216,8,12,128]{3,2,1,0:T(8,128)(2,1)S(1)} %bitcast.74), kind=kOutput, calls=%fused_computation.2.clone.1 | convolution fusion | flops 679477248 | bytes 6586368 | tf_op jit(solution)/shard_map/while/body/eval_jaxpr/dot_general | solution.py:84
  20.9 1.4 broadcast_compare_fusion.4
  22.4 5.9 %select_select_fusion.3 = (bf16[27,64,12,128]{3,2,1,0:T(8,128)(2,1)}, bf16[27,64,12,128]{3,2,1,0:T(8,128)(2,1)S(1)}) fusion(pred[64,12,128]{2,1,0:T(8,128)(4,1)S(1)} %get-tuple-element.305, pred[64,12,128]{2,1,0:T(8,128)(4,1)S(1)} %get-tuple-element.306, pred[64,12,128]{2,1,0:T(8,128)(4,1)S(1)} %get-tuple-element.307, ...), kind=kLoop, calls=%fused_computation.1.clone.1 | loop fusion | flops 15925248 | bytes 10939392 | tf_op jit(solution)/shard_map/while/body/eval_jaxpr/jit(_where)/select_n | solution.py:53
  29.4 4.6 %fusion.46 = f32[1728,128]{1,0:T(8,128)S(1)} fusion(bf16[1536,128]{1,0:T(8,128)(2,1)S(1)} %bitcast.77, bf16[216,8,12,128]{3,2,1,0:T(8,128)(2,1)} %bitcast.75), kind=kOutput, calls=%fused_computation.5.clone.1 | convolution fusion | flops 679477248 | bytes 6586368 | tf_op jit(solution)/shard_map/while/body/eval_jaxpr/dot_general | solution.py:83
  34.0 1.6 %fusion.45 = f32[1728,128]{1,0:T(8,128)S(1)} fusion(bf16[1536,128]{1,0:T(8,128)(2,1)S(1)} %bitcast.78, bf16[216,8,12,128]{3,2,1,0:T(8,128)(2,1)S(1)} %bitcast.74), kind=kOutput, calls=%fused_computation.2.clone.1 | convolution fusion | flops 679477248 | bytes 6586368 | tf_op jit(solution)/shard_map/while/body/eval_jaxpr/dot_general | solution.py:84
  37.1 1.4 broadcast_compare_fusion.4
  38.5 5.9 %select_select_fusion.3 = (bf16[27,64,12,128]{3,2,1,0:T(8,128)(2,1)}, bf16[27,64,12,128]{3,2,1,0:T(8,128)(2,1)S(1)}) fusion(pred[64,12,128]{2,1,0:T(8,128)(4,1)S(1)} %get-tuple-element.305, pred[64,12,128]{2,1,0:T(8,128)(4,1)S(1)} %get-tuple-element.306, pred[64,12,128]{2,1,0:T(8,128)(4,1)S(1)} %get-tuple-element.307, ...), kind=kLoop, calls=%fused_computation.1.clone.1 | loop fusion | flops 15925248 | bytes 10939392 | tf_op jit(solution)/shard_map/while/body/eval_jaxpr/jit(_where)/select_n | solution.py:53
  45.5 4.6 %fusion.46 = f32[1728,128]{1,0:T(8,128)S(1)} fusion(bf16[1536,128]{1,0:T(8,128)(2,1)S(1)} %bitcast.77, bf16[216,8,12,128]{3,2,1,0:T(8,128)(2,1)} %bitcast.75), kind=kOutput, calls=%fused_computation.5.clone.1 | convolution fusion | flops 679477248 | bytes 6586368 | tf_op jit(solution)/shard_map/while/body/eval_jaxpr/dot_general | solution.py:83
  50.1 1.6 %fusion.45 = f32[1728,128]{1,0:T(8,128)S(1)} fusion(bf16[1536,128]{1,0:T(8,128)(2,1)S(1)} %bitcast.78, bf16[216,8,12,128]{3,2,1,0:T(8,128)(2,1)S(1)} %bitcast.74), kind=kOutput, calls=%fused_computation.2.clone.1 | convolution fusion | flops 679477248 | bytes 6586368 | tf_op jit(solution)/shard_map/while/body/eval_jaxpr/dot_general | solution.py:84
  53.2 1.4 broadcast_compare_fusion.4
  54.6 5.9 %select_select_fusion.3 = (bf16[27,64,12,128]{3,2,1,0:T(8,128)(2,1)}, bf16[27,64,12,128]{3,2,1,0:T(8,128)(2,1)S(1)}) fusion(pred[64,12,128]{2,1,0:T(8,128)(4,1)S(1)} %get-tuple-element.305, pred[64,12,128]{2,1,0:T(8,128)(4,1)S(1)} %get-tuple-element.306, pred[64,12,128]{2,1,0:T(8,128)(4,1)S(1)} %get-tuple-element.307, ...), kind=kLoop, calls=%fused_computation.1.clone.1 | loop fusion | flops 15925248 | bytes 10939392 | tf_op jit(solution)/shard_map/while/body/eval_jaxpr/jit(_where)/select_n | solution.py:53
  61.6 4.6 %fusion.46 = f32[1728,128]{1,0:T(8,128)S(1)} fusion(bf16[1536,128]{1,0:T(8,128)(2,1)S(1)} %bitcast.77, bf16[216,8,12,128]{3,2,1,0:T(8,128)(2,1)} %bitcast.75), kind=kOutput, calls=%fused_computation.5.clone.1 | convolution fusion | flops 679477248 | bytes 6586368 | tf_op jit(solution)/shard_map/while/body/eval_jaxpr/dot_general | solution.py:83
  66.2 1.6 %fusion.45 = f32[1728,128]{1,0:T(8,128)S(1)} fusion(bf16[1536,128]{1,0:T(8,128)(2,1)S(1)} %bitcast.78, bf16[216,8,12,128]{3,2,1,0:T(8,128)(2,1)S(1)} %bitcast.74), kind=kOutput, calls=%fused_computation.2.clone.1 | convolution fusion | flops 679477248 | bytes 6586368 | tf_op jit(solution)/shard_map/while/body/eval_jaxpr/dot_general | solution.py:84
  69.7 1.8 %reshape.564 = f32[32,1,6912]{2,1,0:T(1,128)S(1)} reshape(f32[32,1,2,27,2,64]{5,4,3,2,1,0:T(2,128)S(1)} %copy.33) | data formatting | bytes 1769472
  71.5 37.3 %all_to_all.15 = f32[32,1,6912]{2,1,0:T(1,128)S(1)} all-to-all(f32[32,1,6912]{2,1,0:T(1,128)S(1)} %reshape.564), channel_id=1, replica_groups=mesh['space'=32,'tm'=8] {'space'}, dimensions={0} | all-to-all | bytes 1769472 | tf_op jit(solution)/shard_map/all_to_all | solution.py:18
  109.4 2.8 %reduce.3 = f32[32,6912]{1,0:T(8,128)S(1)} reduce(f32[32,1,6912]{2,1,0:T(1,128)S(1)} %all_to_all.15, f32[]{:T(128)} %broadcast.901), dimensions={1}, to_apply=%all_to_all.9.reduce_sub_computation | reduce | bytes 1769476 | tf_op jit(solution)/shard_map/all_to_all | solution.py:18
  115.4 4.1 %all-to-all-start.1 = ((f32[8,1,6912]{2,1,0:T(1,128)}), f32[8,1,6912]{2,1,0:T(1,128)S(1)}, u32[]{:S(2)}, u32[]{:S(2)}) async-start(f32[8,1,6912]{2,1,0:T(1,128)} %reshape.566), calls=%async_computation.1 | async-start | bytes 442368 | tf_op jit(solution)/shard_map/all_to_all | solution.py:24
  119.6 5.6 %all-to-all-done.1 = f32[8,1,6912]{2,1,0:T(1,128)S(1)} async-done(((f32[8,1,6912]{2,1,0:T(1,128)}), f32[8,1,6912]{2,1,0:T(1,128)S(1)}, u32[]{:S(2)}, u32[]{:S(2)}) %all-to-all-start.1) | async-done | bytes 221216 | tf_op jit(solution)/shard_map/all_to_all | solution.py:24
  128.1 17.5 %all_to_all.16 = f32[32,1,432]{2,1,0:T(1,128)S(1)} all-to-all(f32[32,1,432]{2,1,0:T(1,128)S(1)} %reshape.568), channel_id=1, replica_groups=mesh['space'=32,'tm'=8] {'space'}, dimensions={0} | all-to-all | bytes 110592 | tf_op jit(solution)/shard_map/all_to_all | solution.py:24
  (62 shorter events, 19.1 us)
Async XLA Ops:
  0.6 3.8 %copy-start.1 = (s32[27,3]{0,1:T(4,128)S(1)}, s32[27,3]{0,1:T(4,128)}, u32[]{:S(2)}) copy-start(s32[27,3]{0,1:T(4,128)} %param.8) | copy-start | bytes 976
  109.4 10.2 %copy-start.2 = (s32[8,2]{0,1:T(2,128)S(1)}, s32[8,2]{0,1:T(2,128)}, u32[]{:S(2)}) copy-start(s32[8,2]{0,1:T(2,128)} %param.9) | copy-start | bytes 196
  114.1 32.6 %copy-start = (f32[2,27,2,64]{3,2,1,0:T(2,128)}, f32[2,27,2,64]{3,2,1,0:T(2,128)S(1)}, u32[]{:S(2)}) copy-start(f32[2,27,2,64]{3,2,1,0:T(2,128)S(1)} %reduce_sum.38) | copy-start | bytes 82948
  115.4 9.8 %all-to-all-start.1 = ((f32[8,1,6912]{2,1,0:T(1,128)}), f32[8,1,6912]{2,1,0:T(1,128)S(1)}, u32[]{:S(2)}, u32[]{:S(2)}) async-start(f32[8,1,6912]{2,1,0:T(1,128)} %reshape.566), calls=%async_computation.1 | async-start | bytes 442368 | tf_op jit(solution)/shard_map/all_to_all | solution.py:24
where the time goes:
time: 148 us; the launch traced here: 147 us
  blocking collectives  54.8 us (37%)
  other arithmetic  41.3 us (28%)
  matrix products  25.4 us (17%)
  local copies, waits for them, and re-layouts  15 us (10%)
  waiting for transfers between devices  5.6 us (4%)
  starting transfers between devices  4.13 us (3%)
    all_to_all x1, blocking collectives, summed_on_arrival(): lax.all_to_all(pieces, axis, split_axis=0, concat_axis=0, tiled=True)  37.3 us
    select_n x4, other arithmetic, phase_weights(): jnp.where(turns == 0, base_re, jnp.where(turns == 1, base_im, jnp.where(t...  23.8 us
    dot_general x4, matrix products, one_block(): left = jnp.dot(weight_re, stacked, preferred_element_type=jnp.float32)  18.3 us
    all_to_all x1, blocking collectives, copy_for_each(): return lax.all_to_all(copies, axis, split_axis=0, concat_axis=0, tiled=True)  17.5 us
    unnamed x16, local copies, waits for them, and re-layouts  9.55 us
    dot_general x4, matrix products, one_block(): right = jnp.dot(weight_im, stacked, preferred_element_type=jnp.float32)  6.3 us
    eq x4, other arithmetic, phase_weights(): turns == 0  5.79 us
    all_to_all x1, waiting for transfers between devices, copy_for_each(): return lax.all_to_all(copies, axis, split_axis=0, concat_axis=0, tiled=True)  5.6 us
  transfers between devices with their start and end apart: 1, of which 1 were waited for; matrix products, arithmetic and copies ran while one was open for 0% of the time, Pallas kernels for 0%

commit v1 on v0

v1 whole, which is shorter than its diff:
```python
import functools
import math

import jax
import jax.numpy as jnp
import numpy as np
from jax import lax
from jax.experimental import pallas as pl
from jax.experimental.pallas import tpu as pltpu
from jax.sharding import Mesh
from jax.sharding import PartitionSpec as P

EXTENT = 48
LANES = 128
SITE_BLOCK = 64
QX = 5
ZY = 16
GROUP = 28
CHUNK = 2 * GROUP


def trig_table():
    angle = (np.arange(LANES) % EXTENT) * (2.0 * np.pi / EXTENT)
    rows = np.stack([np.cos(angle), np.sin(angle)]).astype(np.float32)
    return np.repeat(rows, 8, axis=0)


def lane_iota(rows):
    return lax.broadcasted_iota(jnp.int32, (rows, LANES), 1)


def looked_up(table, index):
    return jnp.take_along_axis(table, index, axis=1)


def field_kernel(where_ref, mom_ref, table_ref, noise_ref, vec_ref, peer_ref, own_ref, phase_re, phase_im, w_ref, v_ref, d_ref, m_ref):
    nmom = mom_ref.shape[0]
    step = pl.program_id(0)
    offset = where_ref[0]
    core = where_ref[1]
    spincol = noise_ref.shape[0]
    half = spincol * SITE_BLOCK
    cos_table = table_ref[0:8, :]
    sin_table = table_ref[8:16, :]
    lane8 = lane_iota(8)
    low8 = lane8 < SITE_BLOCK
    low64 = lane_iota(64) < SITE_BLOCK

    @pl.when(step == 0)
    def _():
        first = offset + SITE_BLOCK * lax.broadcasted_iota(jnp.int32, (8, LANES), 0)
        line = first // EXTENT + jnp.where(low8, 0, 1)
        y, z = (lax.rem(line, EXTENT), lax.div(line, EXTENT))

        def per_momentum(q, carry):
            index = mom_ref[q, 1] * y + mom_ref[q, 2] * z
            index = jnp.where(index < 0, index + 3 * EXTENT, index)
            index = jnp.where(index >= 2 * EXTENT, index - 2 * EXTENT, index)
            phase_re[q] = looked_up(cos_table, index)
            phase_im[q] = -looked_up(sin_table, index)
            return carry

        lax.fori_loop(0, nmom, per_momentum, 0)
        m_ref[...] = jnp.zeros_like(m_ref)
        zero = jnp.zeros((ZY, LANES), jnp.float32)
        for out in (peer_ref, own_ref):
            for b in range(2):
                out[pl.ds(b * GROUP + GROUP - 1, ZY, stride=CHUNK), :] = zero

    bounds, waves = ([], [])
    for g in range(2):
        first = offset + step * 2 * SITE_BLOCK + g * SITE_BLOCK
        into = lax.rem(first, EXTENT)
        bounds.append(EXTENT - into)
        x = into + (lane8 & (SITE_BLOCK - 1))
        x = jnp.where(x >= EXTENT, x - EXTENT, x)
        x2 = 2 * x
        x2 = jnp.where(x2 >= EXTENT, x2 - EXTENT, x2)
        waves.append([looked_up(t, i)[0:1, :].astype(jnp.bfloat16) for i in (x, x2) for t in (cos_table, sin_table)])

    one = jnp.bfloat16(1)
    two = jnp.bfloat16(2)
    for pair in range(spincol // 2):
        rows = []
        for a in (2 * pair, 2 * pair + 1):
            parts = [noise_ref[a, pl.ds(c * 2 + b, ZY, stride=4), :] for c in (1 - core, core) for b in range(2)]
            rows.append(jnp.concatenate(parts, axis=0))
        turned = [pltpu.roll(r, SITE_BLOCK, 1) for r in rows]
        blocks = (jnp.where(low64, rows[0], turned[1]), jnp.where(low64, turned[0], rows[1]))
        cols = pl.ds(pair * LANES, LANES)
        cols_im = pl.ds(half + pair * LANES, LANES)
        for g in range(2):
            turns = blocks[g].astype(jnp.float32).astype(jnp.bfloat16)
            er = jnp.abs(turns - two) - one
            ei = one - jnp.abs(turns - one)
            w_ref[g, 2 * 64 : 3 * 64, cols] = er
            w_ref[g, 2 * 64 : 3 * 64, cols_im] = -ei
            for k in (1, 2):
                c, s = waves[g][2 * (k - 1) : 2 * k]
                erc, eis, ers, eic = (er * c, ei * s, er * s, ei * c)
                up, down = ((2 + k) * 64, (2 - k) * 64)
                w_ref[g, up : up + 64, cols] = erc - eis
                w_ref[g, up : up + 64, cols_im] = -(ers + eic)
                w_ref[g, down : down + 64, cols] = erc + eis
                w_ref[g, down : down + 64, cols_im] = ers - eic

    site = lax.broadcasted_iota(jnp.int32, (SITE_BLOCK, LANES), 0)
    for g in range(2):
        mask = jnp.where((site < bounds[g]) == low64, 1.0, 0.0).astype(jnp.bfloat16)
        for a in range(spincol):
            v = vec_ref[a, g * SITE_BLOCK : (g + 1) * SITE_BLOCK, :]
            re = jnp.concatenate([v[:, :SITE_BLOCK], v[:, :SITE_BLOCK]], axis=1) * mask
            im = jnp.concatenate([v[:, SITE_BLOCK:], v[:, SITE_BLOCK:]], axis=1) * mask
            k0, k1 = (a * SITE_BLOCK, half + a * SITE_BLOCK)
            v_ref[g, k0 : k0 + SITE_BLOCK, 0:LANES] = re
            v_ref[g, k0 : k0 + SITE_BLOCK, LANES:] = im
            v_ref[g, k1 : k1 + SITE_BLOCK, 0:LANES] = -im
            v_ref[g, k1 : k1 + SITE_BLOCK, LANES:] = re

    for g in range(2):
        d_ref[g] = jnp.dot(w_ref[g], v_ref[g], preferred_element_type=jnp.float32)

    def add_momentum(q, carry):
        row = pl.multiple_of((mom_ref[q, 0] + 2) * 64, 64)
        re, im = (m_ref[q, 0], m_ref[q, 1])
        for g in range(2):
            fr = phase_re[q, pl.ds(step * 2 + g, 1), :]
            fi = phase_im[q, pl.ds(step * 2 + g, 1), :]
            dr = d_ref[g, pl.ds(row, 64), 0:LANES]
            di = d_ref[g, pl.ds(row, 64), LANES:]
            re = re + (fr * dr - fi * di)
            im = im + (fr * di + fi * dr)
        m_ref[q, 0] = re
        m_ref[q, 1] = im
        return carry

    lax.fori_loop(0, nmom, add_momentum, 0)

    @pl.when(step == pl.num_programs(0) - 1)
    def _():
        def finish(q, carry):
            re, im = (m_ref[q, 0], m_ref[q, 1])
            kept = jnp.where(low64, re, im)
            moved = pltpu.roll(jnp.where(low64, im, re), SITE_BLOCK, 1)
            total = kept + moved
            for n, out in enumerate((peer_ref, own_ref)):
                for b in range(2):
                    r = n * 32 + b * ZY
                    out[pl.ds(b * GROUP + q, ZY, stride=CHUNK), :] = total[r : r + ZY]
            return carry

        lax.fori_loop(0, nmom, finish, 0)


def partial_fields(where, momenta, noise, vectors):
    nmom = momenta.shape[0]
    spincol, nvec, sites = noise.shape
    smem = pl.BlockSpec(memory_space=pltpu.SMEM)
    out = jax.ShapeDtypeStruct((ZY * CHUNK, LANES), jnp.float32)
    out_spec = pl.BlockSpec((ZY * CHUNK, LANES), lambda s: (0, 0))
    depth = 2 * spincol * SITE_BLOCK
    return pl.pallas_call(
        field_kernel,
        grid=(sites // LANES,),
        in_specs=[
            smem,
            smem,
            pl.BlockSpec((16, LANES), lambda s: (0, 0)),
            pl.BlockSpec((spincol, nvec, LANES), lambda s: (0, 0, s)),
            pl.BlockSpec((spincol, LANES, LANES), lambda s: (0, s, 0)),
        ],
        out_specs=[out_spec, out_spec],
        out_shape=[out, out],
        scratch_shapes=[
            pltpu.VMEM((nmom, 8, LANES), jnp.float32),
            pltpu.VMEM((nmom, 8, LANES), jnp.float32),
            pltpu.VMEM((2, QX * nvec, depth), jnp.bfloat16),
            pltpu.VMEM((2, depth, 2 * LANES), jnp.bfloat16),
            pltpu.VMEM((2, QX * nvec, 2 * LANES), jnp.float32),
            pltpu.VMEM((nmom, 2, nvec, LANES), jnp.float32),
        ],
        name="fields",
    )(where, momenta, jnp.asarray(trig_table()), noise, vectors)


def mesons_kernel(scale, part_ref, copies_ref, out_ref, row_ref):
    total = part_ref[0]
    for n in range(1, part_ref.shape[0]):
        total = total + part_ref[n]
    total = total * scale
    for n in range(copies_ref.shape[0]):
        copies_ref[n] = total
    row_ref[...] = total
    for q in range(out_ref.shape[2]):
        for b in range(2):
            r = b * GROUP + q
            for c in range(2):
                out_ref[0, c, q, b : b + 1, :] = row_ref[r : r + 1, c * 64 : (c + 1) * 64]


def summed_mesons(parts, scale, copies, nmom):
    return pl.pallas_call(
        functools.partial(mesons_kernel, scale),
        out_shape=[
            jax.ShapeDtypeStruct((copies, CHUNK, LANES), jnp.float32),
            jax.ShapeDtypeStruct((1, 2, nmom, 2, 64), jnp.float32),
        ],
        scratch_shapes=[pltpu.VMEM((CHUNK, LANES), jnp.float32)],
        name="mesons",
    )(parts)


def traces_kernel(pairs_ref, fields_ref, out_ref):
    lane = lane_iota(CHUNK)
    sign = jnp.where(lane < 64, -1.0, 1.0)
    re = jnp.zeros((LANES, LANES), jnp.float32)
    re = jnp.zeros((CHUNK, LANES), jnp.float32)
    im = re
    for k in range(pairs_ref.shape[0]):
        source = fields_ref[pairs_ref[k, 0]]
        sink = fields_ref[pairs_ref[k, 1]]
        swapped = pltpu.roll(source, 64, 1) * sign
        re = jnp.where(lane == k, jnp.sum(sink * source, axis=1, keepdims=True), re)
        im = jnp.where(lane == k, jnp.sum(sink * swapped, axis=1, keepdims=True), im)
    pad = jnp.zeros((64 - CHUNK, LANES), jnp.float32)
    both = jnp.concatenate([re, pad, im, pad], axis=0)
    out_ref[...] = both.T[0:8, :]


def partial_traces(pairs, fields):
    smem = pl.BlockSpec(memory_space=pltpu.SMEM)
    return pl.pallas_call(
        traces_kernel,
        in_specs=[smem, pl.BlockSpec(memory_space=pltpu.VMEM)],
        out_shape=jax.ShapeDtypeStruct((8, LANES), jnp.float32),
        name="traces",
    )(pairs, fields)


def correlators_kernel(factor, part_ref, out_ref):
    total = part_ref[0]
    for n in range(1, part_ref.shape[0]):
        total = total + part_ref[n]
    total = total * factor
    nmom = out_ref.shape[2]
    total = total + pltpu.roll(total, LANES - GROUP, 1)
    moved = pltpu.roll(total, 64, 1)
    for k in range(out_ref.shape[0]):
        out_ref[k, 0:1, :] = total[k : k + 1, 0:nmom]
        out_ref[k, 1:2, :] = moved[k : k + 1, 0:nmom]


def summed_traces(parts, factor, npairs, nmom):
    return pl.pallas_call(
        functools.partial(correlators_kernel, factor),
        out_shape=jax.ShapeDtypeStruct((npairs, 2, nmom), jnp.float32),
        name="correlators",
    )(parts)


def exchange(array, axis):
    return lax.all_to_all(array, axis, split_axis=0, concat_axis=0, tiled=True)


def local(solutions, noise, momenta, pairs):
    spincol, sites, width = solutions.shape[1:]
    nmom = momenta.shape[0]
    core = lax.axis_index("core")
    place = lax.axis_index(("z", "yh", "core"))
    where = jnp.stack([place * sites, core]).astype(jnp.int32)
    peer, own = partial_fields(where, momenta, jnp.swapaxes(noise[0], 0, 1), solutions[0])
    arrived = lax.ppermute(peer, "core", [(0, 1), (1, 0)])
    chunks = (own + arrived).reshape(ZY, CHUNK, LANES)
    scale = 1.0 / math.sqrt(spincol * sites * 2 * ZY)
    copies, mesons = summed_mesons(exchange(chunks, ("z", "yh")), scale, lax.axis_size("tm"), nmom)
    traces = partial_traces(pairs, exchange(copies, "tm"))
    traces = traces + lax.ppermute(traces, "core", [(0, 1), (1, 0)])
    spread = jnp.broadcast_to(traces, (ZY, *traces.shape))
    correlators = summed_traces(exchange(spread, ("z", "yh")), 1.0 / 64, pairs.shape[0], nmom)
    return (mesons, correlators)


def solution(mesh):
    split = Mesh(mesh.devices.reshape(8, 2, 2, 8), ("z", "yh", "core", "tm"))
    space = ("z", "yh", "core")
    in_specs = (P("tm", None, space, None), P("tm", None, None, space), P(), P("tm", None))
    out_specs = (P("tm", None, None, space, None), P("tm", None, None))
    return jax.shard_map(local, mesh=split, in_specs=in_specs, out_specs=out_specs, check_vma=False)
```

time: 148 us -> 83.3 us (0.56)
  other arithmetic: 41.3 us -> 2.44 us
  matrix products: 25.4 us -> 0 us
  Pallas kernels: 0 us -> 20.1 us
  blocking collectives: 54.8 us -> 38 us
  local copies, waits for them, and re-layouts: 15 us -> 2.75 us
  starting transfers between devices: 4.13 us -> 11.3 us
  waiting for transfers between devices: 5.6 us -> 7.66 us
    dot_general x10 -> x0, matrix products: 25.4 us -> none  [the longest x4 18.3 us: one_block(): left = jnp.dot(weight_re, stacked, preferred_element_type=jnp.float32)]
    select_n x12 -> x0, other arithmetic: 23.9 us -> none  [the longest x4 23.8 us: phase_weights(): jnp.where(turns == 0, base_re, jnp.where(turns == 1, base_im, jnp.where(t...]
    pallas_call x0 -> x4, Pallas kernels: none -> 20.1 us  [the longest x1 14.5 us: partial_fields(): pl.pallas_call(field_kernel, grid=(sites // LANES,), in_specs=[smem, smem...]
    all_to_all x2, blocking collectives: 54.8 us -> 38 us  [exchange(): return lax.all_to_all(array, axis, split_axis=0, concat_axis=0, tiled=True)]
    ppermute x0 -> x2, starting transfers between devices: none -> 7.2 us  [the longest x1 4 us: local(): traces = traces + lax.ppermute(traces, 'core', [(0, 1), (1, 0)])]
    unnamed x16 -> x6, local copies, waits for them, and re-layouts: 9.55 us -> 2.74 us
    eq x4 -> x0, other arithmetic: 5.79 us -> none  [phase_weights(): turns == 0]
    all_to_all x3 -> x0, other arithmetic: 4.71 us -> none  [the longest x1 2.75 us: summed_on_arrival(): lax.all_to_all(pieces, axis, split_axis=0, concat_axis=0, tiled=True)]
  transfers between devices with their start and end apart: 1 -> 3, of which waited for: 1 -> 3; matrix products, arithmetic and copies ran while one was open for 0% -> 1% of each run, Pallas kernels for 0% -> 0%
where the time goes in v1:
time: 83.3 us; the launch traced here: 82.9 us
  blocking collectives  38 us (46%)
  Pallas kernels  20.1 us (24%)
  starting transfers between devices  11.3 us (14%)
  waiting for transfers between devices  7.66 us (9%)
  local copies, waits for them, and re-layouts  2.75 us (3%)
  other arithmetic  2.44 us (3%)
    all_to_all x2, blocking collectives, exchange(): return lax.all_to_all(array, axis, split_axis=0, concat_axis=0, tiled=True)  38 us
    pallas_call x1, Pallas kernels, partial_fields(): pl.pallas_call(field_kernel, grid=(sites // LANES,), in_specs=[smem, smem...  14.5 us
    all_to_all x1, waiting for transfers between devices, exchange(): return lax.all_to_all(array, axis, split_axis=0, concat_axis=0, tiled=True)  4.97 us
    all_to_all x1, starting transfers between devices, exchange(): return lax.all_to_all(array, axis, split_axis=0, concat_axis=0, tiled=True)  4.12 us
    ppermute x1, starting transfers between devices, local(): traces = traces + lax.ppermute(traces, 'core', [(0, 1), (1, 0)])  4 us
    ppermute x1, starting transfers between devices, local(): arrived = lax.ppermute(peer, 'core', [(0, 1), (1, 0)])  3.2 us
    unnamed x6, local copies, waits for them, and re-layouts  2.74 us
    pallas_call x1, Pallas kernels, partial_traces(): pl.pallas_call(traces_kernel, in_specs=[smem, pl.BlockSpec(memory_space=p...  2.21 us
  transfers between devices with their start and end apart: 3, of which 3 were waited for; matrix products, arithmetic and copies ran while one was open for 1% of the time, Pallas kernels for 0%

profile of v1, /device:TPU:1, one launch (start us, length us, event | category | flops | bytes accessed | tf_op | source)
XLA Modules:
  0.0 82.9 jit_solution(16817864324322315571)
XLA Ops:
  0.6 1.4 %copy.7.mom_ref = s32[27,3]{1,0:T(8,128)} copy(s32[27,3]{0,1:T(4,128)} %param.7) | data formatting | bytes 648 | tf_op args[2]
  2.0 0.7 pad_add_fusion.where_ref
  2.7 14.5 %fields.1 = (f32[896,128]{1,0:T(8,128)}, f32[896,128]{1,0:T(8,128)}) custom-call(s32[2]{0:T(128)} %pad_add_fusion.where_ref, s32[27,3]{1,0:T(8,128)} %copy.7.mom_ref, f32[16,128]{1,0:T(8,128)} %constant.23.clone.table_ref, s32[12,64,512]{2,1,0:T(8,128)} %bitcast.8, bf16[12,512,128]{2,1,0:T(8,128)(2,1)} %bitcast.9), custom_call_target="tpu_custom_call" | custom-call | tf_op jit(solution)/shard_map/fields/pallas_call | solution.py:162
  17.1 3.2 %collective-permute-start = (f32[896,128]{1,0:T(8,128)}, f32[896,128]{1,0:T(8,128)S(1)}, u32[]{:S(2)}, u32[]{:S(2)}) collective-permute-start(f32[896,128]{1,0:T(8,128)} %get-tuple-element.7), channel_id=1, source_target_pairs={{0,8},{8,0},{1,9},{9,1},{2,10},{10,2},{3,11},{11,3},{4,12},{12,4},... | collective-permute-start | bytes 1376264 | tf_op jit(solution)/shard_map/ppermute | solution.py:272
  20.3 1.7 %collective-permute-done = f32[896,128]{1,0:T(8,128)S(1)} collective-permute-done((f32[896,128]{1,0:T(8,128)}, f32[896,128]{1,0:T(8,128)S(1)}, u32[]{:S(2)}, u32[]{:S(2)}) %collective-permute-start) | collective-permute-done | bytes 458784 | tf_op jit(solution)/shard_map/ppermute | solution.py:272
  22.0 0.0 copy-start.1
  22.0 1.1 %add.14 = f32[896,128]{1,0:T(8,128)S(1)} add(f32[896,128]{1,0:T(8,128)} %get-tuple-element.6, f32[896,128]{1,0:T(8,128)S(1)} %collective-permute-done) | non-fusion elementwise | flops 114688 | bytes 1376256 | tf_op jit(solution)/shard_map/add | solution.py:273
  23.1 25.3 %all_to_all.15.part_ref = f32[16,56,128]{2,1,0:T(8,128)} all-to-all(f32[16,56,128]{2,1,0:T(8,128)S(1)} %bitcast.7), channel_id=1, replica_groups=mesh['z'=8,'yh'=2,'core'=2,'tm'=8] {'z','yh'}, dimensions={0} | all-to-all | bytes 917504 | tf_op jit(solution)/shard_map/all_to_all | solution.py:262
  48.4 1.8 %mesons.1 = (f32[8,56,128]{2,1,0:T(8,128)}, f32[1,2,27,2,64]{4,3,2,1,0:T(2,128)}) custom-call(f32[16,56,128]{2,1,0:T(8,128)} %all_to_all.15.part_ref), custom_call_target="tpu_custom_call" | custom-call | tf_op jit(solution)/shard_map/mesons/pallas_call | solution.py:202
  50.2 4.1 %all-to-all-start.1 = ((f32[8,56,128]{2,1,0:T(8,128)}), f32[8,56,128]{2,1,0:T(8,128)S(1)}, u32[]{:S(2)}, u32[]{:S(2)}) async-start(f32[8,56,128]{2,1,0:T(8,128)} %get-tuple-element.9), calls=%async_computation.1 | async-start | bytes 458752 | tf_op jit(solution)/shard_map/all_to_all | solution.py:262
  54.3 0.0 copy-done.1
  54.3 0.7 copy.8.pairs_ref
  55.0 5.0 %all-to-all-done.1.fields_ref = f32[8,56,128]{2,1,0:T(8,128)S(1)} async-done(((f32[8,56,128]{2,1,0:T(8,128)}), f32[8,56,128]{2,1,0:T(8,128)S(1)}, u32[]{:S(2)}, u32[]{:S(2)}) %all-to-all-start.1) | async-done | bytes 229408 | tf_op jit(solution)/shard_map/all_to_all | solution.py:262
  60.0 0.0 copy-start
  60.0 0.7 copy-done
  60.7 2.2 %traces.1 = f32[8,128]{1,0:T(8,128)} custom-call(s32[8,2]{1,0:T(8,128)} %copy.8.pairs_ref, f32[8,56,128]{2,1,0:T(8,128)} %copy-done), custom_call_target="tpu_custom_call" | custom-call | tf_op jit(solution)/shard_map/traces/pallas_call | solution.py:232
  62.9 4.0 %collective-permute-start.1 = (f32[8,128]{1,0:T(8,128)}, f32[8,128]{1,0:T(8,128)S(1)}, u32[]{:S(2)}, u32[]{:S(2)}) collective-permute-start(f32[8,128]{1,0:T(8,128)} %traces.1), channel_id=1, source_target_pairs={{0,8},{8,0},{1,9},{9,1},{2,10},{10,2},{3,11},{11,3},{4,12},{12,4},... | collective-permute-start | bytes 12296 | tf_op jit(solution)/shard_map/ppermute | solution.py:277
  66.9 1.0 %collective-permute-done.1 = f32[8,128]{1,0:T(8,128)S(1)} collective-permute-done((f32[8,128]{1,0:T(8,128)}, f32[8,128]{1,0:T(8,128)S(1)}, u32[]{:S(2)}, u32[]{:S(2)}) %collective-permute-start.1) | collective-permute-done | bytes 4128 | tf_op jit(solution)/shard_map/ppermute | solution.py:277
  67.9 0.7 add.15
  68.6 12.7 %all_to_all.16.part_ref = f32[16,8,128]{2,1,0:T(8,128)} all-to-all(f32[16,8,128]{2,1,0:T(8,128)S(1)} %broadcast_in_dim.3), channel_id=1, replica_groups=mesh['z'=8,'yh'=2,'core'=2,'tm'=8] {'z','yh'}, dimensions={0} | all-to-all | bytes 131072 | tf_op jit(solution)/shard_map/all_to_all | solution.py:262
  81.3 1.6 %correlators.1 = f32[8,2,27]{2,1,0:T(2,128)} custom-call(f32[16,8,128]{2,1,0:T(8,128)} %all_to_all.16.part_ref), custom_call_target="tpu_custom_call" | custom-call | tf_op jit(solution)/shard_map/correlators/pallas_call | solution.py:254
  (1 shorter events, 0.0 us)
Async XLA Ops:
  17.1 4.9 %collective-permute-start = (f32[896,128]{1,0:T(8,128)}, f32[896,128]{1,0:T(8,128)S(1)}, u32[]{:S(2)}, u32[]{:S(2)}) collective-permute-start(f32[896,128]{1,0:T(8,128)} %get-tuple-element.7), channel_id=1, source_target_pairs={{0,8},{8,0},{1,9},{9,1},{2,10},{10,2},{3,11},{11,3},{4,12},{12,4},... | collective-permute-start | bytes 1376264 | tf_op jit(solution)/shard_map/ppermute | solution.py:272
  22.0 32.3 %copy-start.1 = (s32[8,2]{0,1:T(2,128)S(1)}, s32[8,2]{0,1:T(2,128)}, u32[]{:S(2)}) copy-start(s32[8,2]{0,1:T(2,128)} %param.8) | copy-start | bytes 196
  50.2 9.8 %all-to-all-start.1 = ((f32[8,56,128]{2,1,0:T(8,128)}), f32[8,56,128]{2,1,0:T(8,128)S(1)}, u32[]{:S(2)}, u32[]{:S(2)}) async-start(f32[8,56,128]{2,1,0:T(8,128)} %get-tuple-element.9), calls=%async_computation.1 | async-start | bytes 458752 | tf_op jit(solution)/shard_map/all_to_all | solution.py:262
  60.0 0.7 copy-start
  62.9 5.0 %collective-permute-start.1 = (f32[8,128]{1,0:T(8,128)}, f32[8,128]{1,0:T(8,128)S(1)}, u32[]{:S(2)}, u32[]{:S(2)}) collective-permute-start(f32[8,128]{1,0:T(8,128)} %traces.1), channel_id=1, source_target_pairs={{0,8},{8,0},{1,9},{9,1},{2,10},{10,2},{3,11},{11,3},{4,12},{12,4},... | collective-permute-start | bytes 12296 | tf_op jit(solution)/shard_map/ppermute | solution.py:277

commit v2 on v1

--- a/solution.py
+++ b/solution.py
@@ -19,6 +19,10 @@
 CHUNK = 2 * GROUP
 
 
+def grant(mebibytes):
+    return pltpu.CompilerParams(vmem_limit_bytes=mebibytes << 20)
+
+
 def trig_table():
     angle = (np.arange(LANES) % EXTENT) * (2.0 * np.pi / EXTENT)
     rows = np.stack([np.cos(angle), np.sin(angle)]).astype(np.float32)
@@ -33,11 +37,11 @@
     return jnp.take_along_axis(table, index, axis=1)
 
 
-def field_kernel(where_ref, mom_ref, table_ref, noise_ref, vec_ref, peer_ref, own_ref, phase_re, phase_im, w_ref, v_ref, d_ref, m_ref):
-    nmom = mom_ref.shape[0]
+def field_kernel(offset_ref, core_ref, mom_ref, table_ref, noise_ref, vec_ref, peer_ref, own_ref, phase_re, phase_im, w_ref, v_ref, d_ref, m_ref):
+    nmom = mom_ref.shape[1]
     step = pl.program_id(0)
-    offset = where_ref[0]
-    core = where_ref[1]
+    offset = offset_ref[0]
+    core = core_ref[0]
     spincol = noise_ref.shape[0]
     half = spincol * SITE_BLOCK
     cos_table = table_ref[0:8, :]
@@ -52,15 +56,12 @@
         line = first // EXTENT + jnp.where(low8, 0, 1)
         y, z = (lax.rem(line, EXTENT), lax.div(line, EXTENT))
 
-        def per_momentum(q, carry):
-            index = mom_ref[q, 1] * y + mom_ref[q, 2] * z
+        for q in range(nmom):
+            index = mom_ref[1, q] * y + mom_ref[2, q] * z
             index = jnp.where(index < 0, index + 3 * EXTENT, index)
             index = jnp.where(index >= 2 * EXTENT, index - 2 * EXTENT, index)
             phase_re[q] = looked_up(cos_table, index)
             phase_im[q] = -looked_up(sin_table, index)
-            return carry
-
-        lax.fori_loop(0, nmom, per_momentum, 0)
         m_ref[...] = jnp.zeros_like(m_ref)
         zero = jnp.zeros((ZY, LANES), jnp.float32)
         for out in (peer_ref, own_ref):
@@ -87,41 +88,43 @@
             rows.append(jnp.concatenate(parts, axis=0))
         turned = [pltpu.roll(r, SITE_BLOCK, 1) for r in rows]
         blocks = (jnp.where(low64, rows[0], turned[1]), jnp.where(low64, turned[0], rows[1]))
-        cols = pl.ds(pair * LANES, LANES)
-        cols_im = pl.ds(half + pair * LANES, LANES)
+        cols, cols_im = (pair, spincol // 2 + pair)
         for g in range(2):
             turns = blocks[g].astype(jnp.float32).astype(jnp.bfloat16)
             er = jnp.abs(turns - two) - one
             ei = one - jnp.abs(turns - one)
-            w_ref[g, 2 * 64 : 3 * 64, cols] = er
-            w_ref[g, 2 * 64 : 3 * 64, cols_im] = -ei
+            w_ref[g, cols, 2 * 64 : 3 * 64] = er
+            w_ref[g, cols_im, 2 * 64 : 3 * 64] = -ei
             for k in (1, 2):
                 c, s = waves[g][2 * (k - 1) : 2 * k]
                 erc, eis, ers, eic = (er * c, ei * s, er * s, ei * c)
                 up, down = ((2 + k) * 64, (2 - k) * 64)
-                w_ref[g, up : up + 64, cols] = erc - eis
-                w_ref[g, up : up + 64, cols_im] = -(ers + eic)
-                w_ref[g, down : down + 64, cols] = erc + eis
-                w_ref[g, down : down + 64, cols_im] = ers - eic
+                w_ref[g, cols, up : up + 64] = erc - eis
+                w_ref[g, cols_im, up : up + 64] = -(ers + eic)
+                w_ref[g, cols, down : down + 64] = erc + eis
+                w_ref[g, cols_im, down : down + 64] = ers - eic
 
     site = lax.broadcasted_iota(jnp.int32, (SITE_BLOCK, LANES), 0)
     for g in range(2):
         mask = jnp.where((site < bounds[g]) == low64, 1.0, 0.0).astype(jnp.bfloat16)
         for a in range(spincol):
             v = vec_ref[a, g * SITE_BLOCK : (g + 1) * SITE_BLOCK, :]
-            re = jnp.concatenate([v[:, :SITE_BLOCK], v[:, :SITE_BLOCK]], axis=1) * mask
-            im = jnp.concatenate([v[:, SITE_BLOCK:], v[:, SITE_BLOCK:]], axis=1) * mask
+            turned = pltpu.roll(v, SITE_BLOCK, 1)
+            re = jnp.where(low64, v, turned) * mask
+            im = jnp.where(low64, turned, v) * mask
             k0, k1 = (a * SITE_BLOCK, half + a * SITE_BLOCK)
-            v_ref[g, k0 : k0 + SITE_BLOCK, 0:LANES] = re
-            v_ref[g, k0 : k0 + SITE_BLOCK, LANES:] = im
-            v_ref[g, k1 : k1 + SITE_BLOCK, 0:LANES] = -im
-            v_ref[g, k1 : k1 + SITE_BLOCK, LANES:] = re
+            v_ref[g, 0, k0 : k0 + SITE_BLOCK, :] = re
+            v_ref[g, 1, k0 : k0 + SITE_BLOCK, :] = im
+            v_ref[g, 0, k1 : k1 + SITE_BLOCK, :] = -im
+            v_ref[g, 1, k1 : k1 + SITE_BLOCK, :] = re
 
     for g in range(2):
-        d_ref[g] = jnp.dot(w_ref[g], v_ref[g], preferred_element_type=jnp.float32)
+        left = jnp.concatenate([w_ref[g, n] for n in range(spincol)], axis=1)
+        right = jnp.concatenate([v_ref[g, 0], v_ref[g, 1]], axis=1)
+        d_ref[g] = jnp.dot(left, right, preferred_element_type=jnp.float32)
 
     def add_momentum(q, carry):
-        row = pl.multiple_of((mom_ref[q, 0] + 2) * 64, 64)
+        row = pl.multiple_of((mom_ref[0, q] + 2) * 64, 64)
         re, im = (m_ref[q, 0], m_ref[q, 1])
         for g in range(2):
             fr = phase_re[q, pl.ds(step * 2 + g, 1), :]
@@ -138,7 +141,7 @@
 
     @pl.when(step == pl.num_programs(0) - 1)
     def _():
-        def finish(q, carry):
+        for q in range(nmom):
             re, im = (m_ref[q, 0], m_ref[q, 1])
             kept = jnp.where(low64, re, im)
             moved = pltpu.roll(jnp.where(low64, im, re), SITE_BLOCK, 1)
@@ -147,13 +150,10 @@
                 for b in range(2):
                     r = n * 32 + b * ZY
                     out[pl.ds(b * GROUP + q, ZY, stride=CHUNK), :] = total[r : r + ZY]
-            return carry
-
-        lax.fori_loop(0, nmom, finish, 0)
-
-
-def partial_fields(where, momenta, noise, vectors):
-    nmom = momenta.shape[0]
+
+
+def partial_fields(offset, core, momenta, noise, vectors):
+    nmom = momenta.shape[1]
     spincol, nvec, sites = noise.shape
     smem = pl.BlockSpec(memory_space=pltpu.SMEM)
     out = jax.ShapeDtypeStruct((ZY * CHUNK, LANES), jnp.float32)
@@ -163,6 +163,7 @@
         field_kernel,
         grid=(sites // LANES,),
         in_specs=[
+            smem,
             smem,
             smem,
             pl.BlockSpec((16, LANES), lambda s: (0, 0)),
@@ -174,13 +175,14 @@
         scratch_shapes=[
             pltpu.VMEM((nmom, 8, LANES), jnp.float32),
             pltpu.VMEM((nmom, 8, LANES), jnp.float32),
-            pltpu.VMEM((2, QX * nvec, depth), jnp.bfloat16),
-            pltpu.VMEM((2, depth, 2 * LANES), jnp.bfloat16),
+            pltpu.VMEM((2, spincol, QX * nvec, LANES), jnp.bfloat16),
+            pltpu.VMEM((2, 2, depth, LANES), jnp.bfloat16),
             pltpu.VMEM((2, QX * nvec, 2 * LANES), jnp.float32),
             pltpu.VMEM((nmom, 2, nvec, LANES), jnp.float32),
         ],
+        compiler_params=grant(16),
         name="fields",
-    )(where, momenta, jnp.asarray(trig_table()), noise, vectors)
+    )(offset, core, momenta, jnp.asarray(trig_table()), noise, vectors)
 
 
 def mesons_kernel(scale, part_ref, copies_ref, out_ref, row_ref):
@@ -206,6 +208,7 @@
             jax.ShapeDtypeStruct((1, 2, nmom, 2, 64), jnp.float32),
         ],
         scratch_shapes=[pltpu.VMEM((CHUNK, LANES), jnp.float32)],
+        compiler_params=grant(4),
         name="mesons",
     )(parts)
 
@@ -213,12 +216,11 @@
 def traces_kernel(pairs_ref, fields_ref, out_ref):
     lane = lane_iota(CHUNK)
     sign = jnp.where(lane < 64, -1.0, 1.0)
-    re = jnp.zeros((LANES, LANES), jnp.float32)
     re = jnp.zeros((CHUNK, LANES), jnp.float32)
     im = re
-    for k in range(pairs_ref.shape[0]):
-        source = fields_ref[pairs_ref[k, 0]]
-        sink = fields_ref[pairs_ref[k, 1]]
+    for k in range(pairs_ref.shape[1]):
+        source = fields_ref[pairs_ref[0, k]]
+        sink = fields_ref[pairs_ref[1, k]]
         swapped = pltpu.roll(source, 64, 1) * sign
         re = jnp.where(lane == k, jnp.sum(sink * source, axis=1, keepdims=True), re)
         im = jnp.where(lane == k, jnp.sum(sink * swapped, axis=1, keepdims=True), im)
@@ -233,6 +235,7 @@
         traces_kernel,
         in_specs=[smem, pl.BlockSpec(memory_space=pltpu.VMEM)],
         out_shape=jax.ShapeDtypeStruct((8, LANES), jnp.float32),
+        compiler_params=grant(4),
         name="traces",
     )(pairs, fields)
 
@@ -254,6 +257,7 @@
     return pl.pallas_call(
         functools.partial(correlators_kernel, factor),
         out_shape=jax.ShapeDtypeStruct((npairs, 2, nmom), jnp.float32),
+        compiler_params=grant(4),
         name="correlators",
     )(parts)
 
@@ -267,13 +271,13 @@
     nmom = momenta.shape[0]
     core = lax.axis_index("core")
     place = lax.axis_index(("z", "yh", "core"))
-    where = jnp.stack([place * sites, core]).astype(jnp.int32)
-    peer, own = partial_fields(where, momenta, jnp.swapaxes(noise[0], 0, 1), solutions[0])
+    offset = (place * sites).astype(jnp.int32).reshape(1)
+    peer, own = partial_fields(offset, core.astype(jnp.int32).reshape(1), momenta.T, jnp.swapaxes(noise[0], 0, 1), solutions[0])
     arrived = lax.ppermute(peer, "core", [(0, 1), (1, 0)])
     chunks = (own + arrived).reshape(ZY, CHUNK, LANES)
     scale = 1.0 / math.sqrt(spincol * sites * 2 * ZY)
     copies, mesons = summed_mesons(exchange(chunks, ("z", "yh")), scale, lax.axis_size("tm"), nmom)
-    traces = partial_traces(pairs, exchange(copies, "tm"))
+    traces = partial_traces(pairs.T, exchange(copies, "tm"))
     traces = traces + lax.ppermute(traces, "core", [(0, 1), (1, 0)])
     spread = jnp.broadcast_to(traces, (ZY, *traces.shape))
     correlators = summed_traces(exchange(spread, ("z", "yh")), 1.0 / 64, pairs.shape[0], nmom)

time: 83.3 us -> 74.2 us (0.89)
  blocking collectives: 38 us -> 47.1 us
  Pallas kernels: 20.1 us -> 12.2 us
  waiting for transfers between devices: 7.66 us -> 2.27 us
  starting transfers between devices: 11.3 us -> 7.33 us
  other arithmetic: 2.44 us -> 0.07 us
  local copies, waits for them, and re-layouts: 2.75 us -> 4.2 us
    all_to_all x2 -> x3, blocking collectives: 38 us -> 47.1 us  [exchange(): return lax.all_to_all(array, axis, split_axis=0, concat_axis=0, tiled=True)]
    pallas_call x1, Pallas kernels: 14.5 us -> 9.46 us  [partial_fields(): pl.pallas_call(field_kernel, grid=(sites // LANES,), in_specs=[smem, smem...]
    all_to_all x1 -> x0, waiting for transfers between devices: 4.97 us -> none  [exchange(): return lax.all_to_all(array, axis, split_axis=0, concat_axis=0, tiled=True)]
    all_to_all x1 -> x0, starting transfers between devices: 4.12 us -> none  [exchange(): return lax.all_to_all(array, axis, split_axis=0, concat_axis=0, tiled=True)]
    unnamed x6 -> x10, local copies, waits for them, and re-layouts: 2.74 us -> 4.19 us
    add x1, other arithmetic: 1.1 us -> 0.07 us  [local(): chunks = (own + arrived).reshape(ZY, CHUNK, LANES)]
    pallas_call x1, Pallas kernels: 1.8 us -> 0.78 us  [summed_mesons(): pl.pallas_call(functools.partial(mesons_kernel, scale), out_shape=[jax.Sh...]
    pallas_call x1, Pallas kernels: 2.21 us -> 1.22 us  [partial_traces(): pl.pallas_call(traces_kernel, in_specs=[smem, pl.BlockSpec(memory_space=p...]
  transfers between devices with their start and end apart: 3 -> 2, of which waited for: 3 -> 2; matrix products, arithmetic and copies ran while one was open for 1% -> 0% of each run, Pallas kernels for 0% -> 0%
where the time goes in v2:
time: 74.2 us; the launch traced here: 73.9 us
  blocking collectives  47.1 us (63%)
  Pallas kernels  12.2 us (16%)
  starting transfers between devices  7.33 us (10%)
  local copies, waits for them, and re-layouts  4.2 us (6%)
  waiting for transfers between devices  2.27 us (3%)
    all_to_all x3, blocking collectives, exchange(): return lax.all_to_all(array, axis, split_axis=0, concat_axis=0, tiled=True)  47.1 us
    pallas_call x1, Pallas kernels, partial_fields(): pl.pallas_call(field_kernel, grid=(sites // LANES,), in_specs=[smem, smem...  9.46 us
    unnamed x10, local copies, waits for them, and re-layouts  4.19 us
    ppermute x1, starting transfers between devices, local(): traces = traces + lax.ppermute(traces, 'core', [(0, 1), (1, 0)])  4.06 us
    ppermute x1, starting transfers between devices, local(): arrived = lax.ppermute(peer, 'core', [(0, 1), (1, 0)])  3.27 us
  transfers between devices with their start and end apart: 2, of which 2 were waited for; matrix products, arithmetic and copies ran while one was open for 0% of the time, Pallas kernels for 0%

profile of v2, /device:TPU:1, one launch (start us, length us, event | category | flops | bytes accessed | tf_op | source)
XLA Modules:
  0.0 73.9 jit_solution(438946402498789934)
XLA Ops:
  0.6 0.0 copy-start
  0.6 1.4 %copy-done = s32[1,64,12,512]{3,1,2,0:T(8,128)S(1)} copy-done((s32[1,64,12,512]{3,1,2,0:T(8,128)S(1)}, s32[1,64,12,512]{3,1,2,0:T(8,128)}, u32[]{:S(2)}) %copy-start) | copy-done | bytes 1572888
  2.0 0.0 copy-start.1
  2.0 1.4 %copy-done.1 = bf16[1,12,512,128]{3,2,1,0:T(8,128)(2,1)S(1)} copy-done((bf16[1,12,512,128]{3,2,1,0:T(8,128)(2,1)S(1)}, bf16[1,12,512,128]{3,2,1,0:T(8,128)(2,1)}, u32[]{:S(2)}) %copy-start.1) | copy-done | bytes 1572888
  3.5 0.0 copy-start.2
  3.5 0.7 copy-done.2
  4.2 0.0 copy-start.3
  4.2 0.7 copy-done.3
  4.8 9.5 %fields.1 = (f32[896,128]{1,0:T(8,128)S(1)}, f32[896,128]{1,0:T(8,128)S(1)}) custom-call(s32[1]{0:T(128)} %bitcast.offset_ref, s32[1]{0:T(128)} %bitcast.1.core_ref, s32[3,27]{1,0:T(4,128)S(1)} %bitcast.11, f32[16,128]{1,0:T(8,128)S(1)} %copy-done.2, s32[12,64,512]{2,1,0:T(8,128)S(1)} %bitcast.9, bf16[12,512,128]{2,1,0:T(8,128)(2,1)S(1)} %bitcast.10), custom_call_target="tpu_custom_call" | custom-call | tf_op jit(solution)/shard_map/fields/pallas_call | solution.py:162
  14.3 3.3 %collective-permute-start = (f32[896,128]{1,0:T(8,128)S(1)}, f32[896,128]{1,0:T(8,128)S(1)}, u32[]{:S(2)}, u32[]{:S(2)}) collective-permute-start(f32[896,128]{1,0:T(8,128)S(1)} %get-tuple-element.7), channel_id=1, source_target_pairs={{0,8},{8,0},{1,9},{9,1},{2,10},{10,2},{3,11},{11,3},{4,12},{12,4},... | collective-permute-start | bytes 1376264 | tf_op jit(solution)/shard_map/ppermute | solution.py:276
  17.6 1.4 %collective-permute-done = f32[896,128]{1,0:T(8,128)S(1)} collective-permute-done((f32[896,128]{1,0:T(8,128)S(1)}, f32[896,128]{1,0:T(8,128)S(1)}, u32[]{:S(2)}, u32[]{:S(2)}) %collective-permute-start) | collective-permute-done | bytes 458784 | tf_op jit(solution)/shard_map/ppermute | solution.py:276
  19.0 0.0 copy-start.4
  19.0 0.1 add.14
  19.1 25.2 %all_to_all.15.part_ref = f32[16,56,128]{2,1,0:T(8,128)S(1)} all-to-all(f32[16,56,128]{2,1,0:T(8,128)S(1)} %bitcast.13), channel_id=1, replica_groups=mesh['z'=8,'yh'=2,'core'=2,'tm'=8] {'z','yh'}, dimensions={0} | all-to-all | bytes 917504 | tf_op jit(solution)/shard_map/all_to_all | solution.py:266
  44.3 0.8 %mesons.1 = (f32[8,56,128]{2,1,0:T(8,128)S(1)}, f32[1,2,27,2,64]{4,3,2,1,0:T(2,128)}) custom-call(f32[16,56,128]{2,1,0:T(8,128)S(1)} %all_to_all.15.part_ref), custom_call_target="tpu_custom_call" | custom-call | tf_op jit(solution)/shard_map/mesons/pallas_call | solution.py:204
  45.1 9.6 %all_to_all.16.fields_ref = f32[8,56,128]{2,1,0:T(8,128)S(1)} all-to-all(f32[8,56,128]{2,1,0:T(8,128)S(1)} %get-tuple-element.9), channel_id=1, replica_groups=mesh['z'=8,'yh'=2,'core'=2,'tm'=8] {'tm'}, dimensions={0} | all-to-all | bytes 458752 | tf_op jit(solution)/shard_map/all_to_all | solution.py:266
  54.7 0.0 copy-done.4
  54.7 1.2 %traces.1 = f32[8,128]{1,0:T(8,128)S(1)} custom-call(s32[2,8]{1,0:T(2,128)S(1)} %bitcast.12, f32[8,56,128]{2,1,0:T(8,128)S(1)} %all_to_all.16.fields_ref), custom_call_target="tpu_custom_call" | custom-call | tf_op jit(solution)/shard_map/traces/pallas_call | solution.py:234
  55.9 4.1 %collective-permute-start.1 = (f32[8,128]{1,0:T(8,128)S(1)}, f32[8,128]{1,0:T(8,128)S(1)}, u32[]{:S(2)}, u32[]{:S(2)}) collective-permute-start(f32[8,128]{1,0:T(8,128)S(1)} %traces.1), channel_id=1, source_target_pairs={{0,8},{8,0},{1,9},{9,1},{2,10},{10,2},{3,11},{11,3},{4,12},{12,4},... | collective-permute-start | bytes 12296 | tf_op jit(solution)/shard_map/ppermute | solution.py:281
  59.9 0.8 %collective-permute-done.1 = f32[8,128]{1,0:T(8,128)S(1)} collective-permute-done((f32[8,128]{1,0:T(8,128)S(1)}, f32[8,128]{1,0:T(8,128)S(1)}, u32[]{:S(2)}, u32[]{:S(2)}) %collective-permute-start.1) | collective-permute-done | bytes 4128 | tf_op jit(solution)/shard_map/ppermute | solution.py:281
  60.8 12.4 %all_to_all.17.part_ref = f32[16,8,128]{2,1,0:T(8,128)S(1)} all-to-all(f32[16,8,128]{2,1,0:T(8,128)S(1)} %broadcast_in_dim.3), channel_id=1, replica_groups=mesh['z'=8,'yh'=2,'core'=2,'tm'=8] {'z','yh'}, dimensions={0} | all-to-all | bytes 131072 | tf_op jit(solution)/shard_map/all_to_all | solution.py:266
  73.1 0.8 %correlators.1 = f32[8,2,27]{2,1,0:T(2,128)} custom-call(f32[16,8,128]{2,1,0:T(8,128)S(1)} %all_to_all.17.part_ref), custom_call_target="tpu_custom_call" | custom-call | tf_op jit(solution)/shard_map/correlators/pallas_call | solution.py:257
  (2 shorter events, 0.0 us)
Async XLA Ops:
  0.6 1.4 %copy-start = (s32[1,64,12,512]{3,1,2,0:T(8,128)S(1)}, s32[1,64,12,512]{3,1,2,0:T(8,128)}, u32[]{:S(2)}) copy-start(s32[1,64,12,512]{3,1,2,0:T(8,128)} %param.6) | copy-start | bytes 4718596
  2.0 1.4 %copy-start.1 = (bf16[1,12,512,128]{3,2,1,0:T(8,128)(2,1)S(1)}, bf16[1,12,512,128]{3,2,1,0:T(8,128)(2,1)}, u32[]{:S(2)}) copy-start(bf16[1,12,512,128]{3,2,1,0:T(8,128)(2,1)} %param.5) | copy-start | bytes 4718596
  3.5 0.7 copy-start.2
  4.2 0.7 copy-start.3
  14.3 4.7 %collective-permute-start = (f32[896,128]{1,0:T(8,128)S(1)}, f32[896,128]{1,0:T(8,128)S(1)}, u32[]{:S(2)}, u32[]{:S(2)}) collective-permute-start(f32[896,128]{1,0:T(8,128)S(1)} %get-tuple-element.7), channel_id=1, source_target_pairs={{0,8},{8,0},{1,9},{9,1},{2,10},{10,2},{3,11},{11,3},{4,12},{12,4},... | collective-permute-start | bytes 1376264 | tf_op jit(solution)/shard_map/ppermute | solution.py:276
  19.0 35.6 %copy-start.4 = (s32[8,2]{0,1:T(2,128)S(1)}, s32[8,2]{0,1:T(2,128)}, u32[]{:S(2)}) copy-start(s32[8,2]{0,1:T(2,128)} %param.8) | copy-start | bytes 196
  55.9 4.9 %collective-permute-start.1 = (f32[8,128]{1,0:T(8,128)S(1)}, f32[8,128]{1,0:T(8,128)S(1)}, u32[]{:S(2)}, u32[]{:S(2)}) collective-permute-start(f32[8,128]{1,0:T(8,128)S(1)} %traces.1), channel_id=1, source_target_pairs={{0,8},{8,0},{1,9},{9,1},{2,10},{10,2},{3,11},{11,3},{4,12},{12,4},... | collective-permute-start | bytes 12296 | tf_op jit(solution)/shard_map/ppermute | solution.py:281

commit v3 on v2

v3 whole, which is shorter than its diff:
```python
import functools
import math

import jax
import jax.numpy as jnp
import numpy as np
from jax import lax
from jax.experimental import pallas as pl
from jax.experimental.pallas import tpu as pltpu
from jax.sharding import Mesh
from jax.sharding import PartitionSpec as P

EXTENT = 48
LANES = 128
SITE_BLOCK = 64
QX = 5
ZY = 16
GROUP = 28
CHUNK = 2 * GROUP


def grant(mebibytes):
    return pltpu.CompilerParams(vmem_limit_bytes=mebibytes << 20)


def trig_table():
    angle = (np.arange(LANES) % EXTENT) * (2.0 * np.pi / EXTENT)
    rows = np.stack([np.cos(angle), np.sin(angle)]).astype(np.float32)
    return np.repeat(rows, 8, axis=0)


def lane_iota(rows):
    return lax.broadcasted_iota(jnp.int32, (rows, LANES), 1)


def looked_up(table, index):
    return jnp.take_along_axis(table, index, axis=1)


def field_kernel(mom_hbm, table_hbm, noise_hbm, vec_hbm, peer_ref, own_ref, mom_ref, table_ref, noise_ref, vec_ref, phase_re, phase_im, d_ref, sems):
    nmom = mom_ref.shape[1]
    steps, spincol, nvec = noise_ref.shape[:3]
    core = lax.axis_index("core")
    place = (lax.axis_index("z") * 2 + lax.axis_index("yh")) * 2 + core
    offset = place * (steps * LANES)

    small = [
        pltpu.make_async_copy(mom_hbm, mom_ref, sems.at[0, 0]),
        pltpu.make_async_copy(table_hbm, table_ref, sems.at[1, 0]),
    ]
    blocks = []
    for step in range(steps):
        span = pl.ds(step * LANES, LANES)
        blocks.append(
            [
                pltpu.make_async_copy(noise_hbm.at[:, :, span], noise_ref.at[step], sems.at[0, step + 1]),
                pltpu.make_async_copy(vec_hbm.at[:, span, :], vec_ref.at[step], sems.at[1, step + 1]),
            ]
        )
    for copy in small + sum(blocks, []):
        copy.start()
    for copy in small:
        copy.wait()

    cos_table = table_ref[0:8, :]
    sin_table = table_ref[8:16, :]
    lane8 = lane_iota(8)
    low8 = lane8 < SITE_BLOCK
    low64 = lane_iota(64) < SITE_BLOCK

    first = offset + SITE_BLOCK * lax.broadcasted_iota(jnp.int32, (8, LANES), 0)
    line = lax.div(first, EXTENT) + jnp.where(low8, 0, 1)
    y, z = (lax.rem(line, EXTENT), lax.div(line, EXTENT))
    for q in range(nmom):
        index = mom_ref[1, q] * y + mom_ref[2, q] * z
        index = jnp.where(index < 0, index + 3 * EXTENT, index)
        index = jnp.where(index >= 2 * EXTENT, index - 2 * EXTENT, index)
        phase_re[q] = looked_up(cos_table, index)
        phase_im[q] = -looked_up(sin_table, index)
    zero = jnp.zeros((ZY, LANES), jnp.float32)
    for out in (peer_ref, own_ref):
        for b in range(2):
            out[pl.ds(b * GROUP + GROUP - 1, ZY, stride=CHUNK), :] = zero

    one = jnp.bfloat16(1)
    two = jnp.bfloat16(2)
    site = lax.broadcasted_iota(jnp.int32, (SITE_BLOCK, LANES), 0)
    for step in range(steps):
        waves, masks = ([], [])
        for g in range(2):
            into = lax.rem(offset + (step * 2 + g) * SITE_BLOCK, EXTENT)
            x = into + (lane8 & (SITE_BLOCK - 1))
            x = jnp.where(x >= EXTENT, x - EXTENT, x)
            x2 = 2 * x
            x2 = jnp.where(x2 >= EXTENT, x2 - EXTENT, x2)
            waves.append([looked_up(t, i)[0:1, :].astype(jnp.bfloat16) for i in (x, x2) for t in (cos_table, sin_table)])
            masks.append(jnp.where((site < EXTENT - into) == low64, 1.0, 0.0).astype(jnp.bfloat16))
        for copy in blocks[step]:
            copy.wait()

        totals = [None, None]
        for pair in range(spincol // 2):
            rows = []
            for a in (2 * pair, 2 * pair + 1):
                parts = [noise_ref[step, a, pl.ds(c * 2 + b, ZY, stride=4), :] for c in (1 - core, core) for b in range(2)]
                rows.append(jnp.concatenate(parts, axis=0))
            turned = [pltpu.roll(r, SITE_BLOCK, 1) for r in rows]
            halves = (jnp.where(low64, rows[0], turned[1]), jnp.where(low64, turned[0], rows[1]))
            for g in range(2):
                turns = halves[g].astype(jnp.float32).astype(jnp.bfloat16)
                er = jnp.abs(turns - two) - one
                ei = one - jnp.abs(turns - one)
                left_re = {2: er}
                left_im = {2: -ei}
                for k in (1, 2):
                    c, s = waves[g][2 * (k - 1) : 2 * k]
                    erc, eis, ers, eic = (er * c, ei * s, er * s, ei * c)
                    left_re[2 + k], left_im[2 + k] = (erc - eis, -(ers + eic))
                    left_re[2 - k], left_im[2 - k] = (erc + eis, ers - eic)
                left = [jnp.concatenate([part[n] for n in range(QX)], axis=0) for part in (left_re, left_im)]
                re, im = ([], [])
                for a in (2 * pair, 2 * pair + 1):
                    v = vec_ref[step, a, g * SITE_BLOCK : (g + 1) * SITE_BLOCK, :]
                    swapped = pltpu.roll(v, SITE_BLOCK, 1)
                    re.append(jnp.where(low64, v, swapped) * masks[g])
                    im.append(jnp.where(low64, swapped, v) * masks[g])
                right = [jnp.concatenate(re + [-i for i in im], axis=0), jnp.concatenate(im + re, axis=0)]
                product = jnp.dot(
                    jnp.concatenate(left, axis=1), jnp.concatenate(right, axis=1), preferred_element_type=jnp.float32
                )
                totals[g] = product if totals[g] is None else totals[g] + product
        for g in range(2):
            d_ref[step * 2 + g] = totals[g]

    low = lane_iota(nvec) < SITE_BLOCK
    for q in range(nmom):
        row = pl.multiple_of((mom_ref[0, q] + 2) * nvec, nvec)
        re = im = jnp.zeros((nvec, LANES), jnp.float32)
        for g in range(2 * steps):
            fr = phase_re[q, g : g + 1, :]
            fi = phase_im[q, g : g + 1, :]
            dr = d_ref[g, pl.ds(row, nvec), 0:LANES]
            di = d_ref[g, pl.ds(row, nvec), LANES:]
            re = re + (fr * dr - fi * di)
            im = im + (fr * di + fi * dr)
        total = jnp.where(low, re, im) + pltpu.roll(jnp.where(low, im, re), SITE_BLOCK, 1)
        for n, out in enumerate((peer_ref, own_ref)):
            for b in range(2):
                r = n * 2 * ZY + b * ZY
                out[pl.ds(b * GROUP + q, ZY, stride=CHUNK), :] = total[r : r + ZY]


def partial_fields(momenta, noise, vectors):
    nmom = momenta.shape[1]
    spincol, nvec, sites = noise.shape
    steps = sites // LANES
    out = pltpu.VMEM((ZY * CHUNK, LANES), jnp.float32)
    return pl.pallas_call(
        field_kernel,
        in_specs=[pl.BlockSpec(memory_space=pltpu.HBM)] * 4,
        out_shape=[out, out],
        scratch_shapes=[
            pltpu.SMEM(momenta.shape, jnp.int32),
            pltpu.VMEM((16, LANES), jnp.float32),
            pltpu.VMEM((steps, spincol, nvec, LANES), jnp.int32),
            pltpu.VMEM((steps, spincol, LANES, LANES), jnp.bfloat16),
            pltpu.VMEM((nmom, 8, LANES), jnp.float32),
            pltpu.VMEM((nmom, 8, LANES), jnp.float32),
            pltpu.VMEM((2 * steps, QX * nvec, 2 * LANES), jnp.float32),
            pltpu.SemaphoreType.DMA((2, steps + 1)),
        ],
        compiler_params=grant(24),
        name="fields",
    )(*[pltpu.with_memory_space_constraint(a, pltpu.HBM) for a in (momenta, jnp.asarray(trig_table()), noise, vectors)])


def mesons_kernel(scale, part_ref, copies_ref, out_ref, row_ref):
    total = part_ref[0]
    for n in range(1, part_ref.shape[0]):
        total = total + part_ref[n]
    total = total * scale
    for n in range(copies_ref.shape[0]):
        copies_ref[n] = total
    row_ref[...] = total
    for q in range(out_ref.shape[2]):
        for b in range(2):
            r = b * GROUP + q
            for c in range(2):
                out_ref[0, c, q, b : b + 1, :] = row_ref[r : r + 1, c * 64 : (c + 1) * 64]


def summed_mesons(parts, scale, copies, nmom):
    return pl.pallas_call(
        functools.partial(mesons_kernel, scale),
        out_shape=[
            jax.ShapeDtypeStruct((copies, CHUNK, LANES), jnp.float32),
            jax.ShapeDtypeStruct((1, 2, nmom, 2, 64), jnp.float32),
        ],
        scratch_shapes=[pltpu.VMEM((CHUNK, LANES), jnp.float32)],
        compiler_params=grant(4),
        name="mesons",
    )(parts)


def traces_kernel(pairs_ref, fields_ref, out_ref):
    lane = lane_iota(CHUNK)
    sign = jnp.where(lane < 64, -1.0, 1.0)
    re = jnp.zeros((CHUNK, LANES), jnp.float32)
    im = re
    for k in range(pairs_ref.shape[1]):
        source = fields_ref[pairs_ref[0, k]]
        sink = fields_ref[pairs_ref[1, k]]
        swapped = pltpu.roll(source, 64, 1) * sign
        re = jnp.where(lane == k, jnp.sum(sink * source, axis=1, keepdims=True), re)
        im = jnp.where(lane == k, jnp.sum(sink * swapped, axis=1, keepdims=True), im)
    pad = jnp.zeros((64 - CHUNK, LANES), jnp.float32)
    both = jnp.concatenate([re, pad, im, pad], axis=0)
    out_ref[...] = both.T[0:8, :]


def partial_traces(pairs, fields):
    smem = pl.BlockSpec(memory_space=pltpu.SMEM)
    return pl.pallas_call(
        traces_kernel,
        in_specs=[smem, pl.BlockSpec(memory_space=pltpu.VMEM)],
        out_shape=jax.ShapeDtypeStruct((8, LANES), jnp.float32),
        compiler_params=grant(4),
        name="traces",
    )(pairs, fields)


def correlators_kernel(factor, part_ref, out_ref):
    total = part_ref[0]
    for n in range(1, part_ref.shape[0]):
        total = total + part_ref[n]
    total = total * factor
    nmom = out_ref.shape[2]
    total = total + pltpu.roll(total, LANES - GROUP, 1)
    moved = pltpu.roll(total, 64, 1)
    for k in range(out_ref.shape[0]):
        out_ref[k, 0:1, :] = total[k : k + 1, 0:nmom]
        out_ref[k, 1:2, :] = moved[k : k + 1, 0:nmom]


def summed_traces(parts, factor, npairs, nmom):
    return pl.pallas_call(
        functools.partial(correlators_kernel, factor),
        out_shape=jax.ShapeDtypeStruct((npairs, 2, nmom), jnp.float32),
        compiler_params=grant(4),
        name="correlators",
    )(parts)


def exchange(array, axis):
    return lax.all_to_all(array, axis, split_axis=0, concat_axis=0, tiled=True)


def local(solutions, noise, momenta, pairs):
    spincol, sites, width = solutions.shape[1:]
    nmom = momenta.shape[0]
    peer, own = partial_fields(momenta.T, jnp.swapaxes(noise[0], 0, 1), solutions[0])
    arrived = lax.ppermute(peer, "core", [(0, 1), (1, 0)])
    chunks = (own + arrived).reshape(ZY, CHUNK, LANES)
    scale = 1.0 / math.sqrt(spincol * sites * 2 * ZY)
    copies, mesons = summed_mesons(exchange(chunks, ("z", "yh")), scale, lax.axis_size("tm"), nmom)
    traces = partial_traces(pairs.T, exchange(copies, "tm"))
    traces = traces + lax.ppermute(traces, "core", [(0, 1), (1, 0)])
    spread = jnp.broadcast_to(traces, (ZY, *traces.shape))
    correlators = summed_traces(exchange(spread, ("z", "yh")), 1.0 / 64, pairs.shape[0], nmom)
    return (mesons, correlators)


def solution(mesh):
    split = Mesh(mesh.devices.reshape(8, 2, 2, 8), ("z", "yh", "core", "tm"))
    space = ("z", "yh", "core")
    in_specs = (P("tm", None, space, None), P("tm", None, None, space), P(), P("tm", None))
    out_specs = (P("tm", None, None, space, None), P("tm", None, None))
    return jax.shard_map(local, mesh=split, in_specs=in_specs, out_specs=out_specs, check_vma=False)
```

time: 74.2 us -> 66.8 us (0.900)
  local copies, waits for them, and re-layouts: 4.2 us -> 0.01 us
  Pallas kernels: 12.2 us -> 9.11 us
    unnamed x10 -> x2, local copies, waits for them, and re-layouts: 4.19 us -> 0.01 us
    pallas_call x1, Pallas kernels: 9.46 us -> 6.36 us  [partial_fields(): pl.pallas_call(field_kernel, in_specs=[pl.BlockSpec(memory_space=pltpu.HB...]
where the time goes in v3:
time: 66.8 us; the launch traced here: 66.6 us
  blocking collectives  47.1 us (71%)
  Pallas kernels  9.11 us (14%)
  starting transfers between devices  7.35 us (11%)
  waiting for transfers between devices  2.27 us (3%)
    all_to_all x3, blocking collectives, exchange(): return lax.all_to_all(array, axis, split_axis=0, concat_axis=0, tiled=True)  47.1 us
    pallas_call x1, Pallas kernels, partial_fields(): pl.pallas_call(field_kernel, in_specs=[pl.BlockSpec(memory_space=pltpu.HB...  6.36 us
    ppermute x1, starting transfers between devices, local(): traces = traces + lax.ppermute(traces, 'core', [(0, 1), (1, 0)])  4.06 us
    ppermute x1, starting transfers between devices, local(): arrived = lax.ppermute(peer, 'core', [(0, 1), (1, 0)])  3.29 us
    ppermute x1, waiting for transfers between devices, local(): arrived = lax.ppermute(peer, 'core', [(0, 1), (1, 0)])  1.44 us
  transfers between devices with their start and end apart: 2, of which 2 were waited for; matrix products, arithmetic and copies ran while one was open for 0% of the time, Pallas kernels for 0%

profile of v3, /device:TPU:1, one launch (start us, length us, event | category | flops | bytes accessed | tf_op | source)
XLA Modules:
  0.0 66.6 jit_solution(14640455389713343452)
XLA Ops:
  0.6 6.4 %fields.1 = (f32[896,128]{1,0:T(8,128)S(1)}, f32[896,128]{1,0:T(8,128)S(1)}) custom-call(s32[3,27]{1,0:T(4,128)} %bitcast.11, f32[16,128]{1,0:T(8,128)} %constant.2.clone.table_hbm, s32[12,64,512]{2,1,0:T(8,128)} %bitcast.9, bf16[12,512,128]{2,1,0:T(8,128)(2,1)} %bitcast.10), custom_call_target="tpu_custom_call" | custom-call | tf_op jit(solution)/shard_map/fields/pallas_call | solution.py:158
  7.0 3.3 %collective-permute-start = (f32[896,128]{1,0:T(8,128)S(1)}, f32[896,128]{1,0:T(8,128)S(1)}, u32[]{:S(2)}, u32[]{:S(2)}) collective-permute-start(f32[896,128]{1,0:T(8,128)S(1)} %get-tuple-element.7), channel_id=1, source_target_pairs={{0,8},{8,0},{1,9},{9,1},{2,10},{10,2},{3,11},{11,3},{4,12},{12,4},... | collective-permute-start | bytes 1376264 | tf_op jit(solution)/shard_map/ppermute | solution.py:262
  10.3 1.4 %collective-permute-done = f32[896,128]{1,0:T(8,128)S(1)} collective-permute-done((f32[896,128]{1,0:T(8,128)S(1)}, f32[896,128]{1,0:T(8,128)S(1)}, u32[]{:S(2)}, u32[]{:S(2)}) %collective-permute-start) | collective-permute-done | bytes 458784 | tf_op jit(solution)/shard_map/ppermute | solution.py:262
  11.7 0.0 copy-start
  11.7 0.1 add.6
  11.8 25.2 %all_to_all.15.part_ref = f32[16,56,128]{2,1,0:T(8,128)S(1)} all-to-all(f32[16,56,128]{2,1,0:T(8,128)S(1)} %bitcast.8), channel_id=1, replica_groups=mesh['z'=8,'yh'=2,'core'=2,'tm'=8] {'z','yh'}, dimensions={0} | all-to-all | bytes 917504 | tf_op jit(solution)/shard_map/all_to_all | solution.py:255
  37.0 0.8 %mesons.1 = (f32[8,56,128]{2,1,0:T(8,128)S(1)}, f32[1,2,27,2,64]{4,3,2,1,0:T(2,128)}) custom-call(f32[16,56,128]{2,1,0:T(8,128)S(1)} %all_to_all.15.part_ref), custom_call_target="tpu_custom_call" | custom-call | tf_op jit(solution)/shard_map/mesons/pallas_call | solution.py:193
  37.8 9.6 %all_to_all.16.fields_ref = f32[8,56,128]{2,1,0:T(8,128)S(1)} all-to-all(f32[8,56,128]{2,1,0:T(8,128)S(1)} %get-tuple-element.9), channel_id=1, replica_groups=mesh['z'=8,'yh'=2,'core'=2,'tm'=8] {'tm'}, dimensions={0} | all-to-all | bytes 458752 | tf_op jit(solution)/shard_map/all_to_all | solution.py:255
  47.3 0.0 copy-done
  47.3 1.2 %traces.1 = f32[8,128]{1,0:T(8,128)S(1)} custom-call(s32[2,8]{1,0:T(2,128)S(1)} %bitcast.7, f32[8,56,128]{2,1,0:T(8,128)S(1)} %all_to_all.16.fields_ref), custom_call_target="tpu_custom_call" | custom-call | tf_op jit(solution)/shard_map/traces/pallas_call | solution.py:223
  48.6 4.1 %collective-permute-start.1 = (f32[8,128]{1,0:T(8,128)S(1)}, f32[8,128]{1,0:T(8,128)S(1)}, u32[]{:S(2)}, u32[]{:S(2)}) collective-permute-start(f32[8,128]{1,0:T(8,128)S(1)} %traces.1), channel_id=1, source_target_pairs={{0,8},{8,0},{1,9},{9,1},{2,10},{10,2},{3,11},{11,3},{4,12},{12,4},... | collective-permute-start | bytes 12296 | tf_op jit(solution)/shard_map/ppermute | solution.py:267
  52.6 0.8 %collective-permute-done.1 = f32[8,128]{1,0:T(8,128)S(1)} collective-permute-done((f32[8,128]{1,0:T(8,128)S(1)}, f32[8,128]{1,0:T(8,128)S(1)}, u32[]{:S(2)}, u32[]{:S(2)}) %collective-permute-start.1) | collective-permute-done | bytes 4128 | tf_op jit(solution)/shard_map/ppermute | solution.py:267
  53.5 12.4 %all_to_all.17.part_ref = f32[16,8,128]{2,1,0:T(8,128)S(1)} all-to-all(f32[16,8,128]{2,1,0:T(8,128)S(1)} %broadcast_in_dim.3), channel_id=1, replica_groups=mesh['z'=8,'yh'=2,'core'=2,'tm'=8] {'z','yh'}, dimensions={0} | all-to-all | bytes 131072 | tf_op jit(solution)/shard_map/all_to_all | solution.py:255
  65.8 0.8 %correlators.1 = f32[8,2,27]{2,1,0:T(2,128)} custom-call(f32[16,8,128]{2,1,0:T(8,128)S(1)} %all_to_all.17.part_ref), custom_call_target="tpu_custom_call" | custom-call | tf_op jit(solution)/shard_map/correlators/pallas_call | solution.py:246
  (2 shorter events, 0.0 us)
Async XLA Ops:
  7.0 4.7 %collective-permute-start = (f32[896,128]{1,0:T(8,128)S(1)}, f32[896,128]{1,0:T(8,128)S(1)}, u32[]{:S(2)}, u32[]{:S(2)}) collective-permute-start(f32[896,128]{1,0:T(8,128)S(1)} %get-tuple-element.7), channel_id=1, source_target_pairs={{0,8},{8,0},{1,9},{9,1},{2,10},{10,2},{3,11},{11,3},{4,12},{12,4},... | collective-permute-start | bytes 1376264 | tf_op jit(solution)/shard_map/ppermute | solution.py:262
  11.7 35.6 %copy-start = (s32[8,2]{0,1:T(2,128)S(1)}, s32[8,2]{0,1:T(2,128)}, u32[]{:S(2)}) copy-start(s32[8,2]{0,1:T(2,128)} %param.8) | copy-start | bytes 196
  48.6 4.9 %collective-permute-start.1 = (f32[8,128]{1,0:T(8,128)S(1)}, f32[8,128]{1,0:T(8,128)S(1)}, u32[]{:S(2)}, u32[]{:S(2)}) collective-permute-start(f32[8,128]{1,0:T(8,128)S(1)} %traces.1), channel_id=1, source_target_pairs={{0,8},{8,0},{1,9},{9,1},{2,10},{10,2},{3,11},{11,3},{4,12},{12,4},... | collective-permute-start | bytes 12296 | tf_op jit(solution)/shard_map/ppermute | solution.py:267

commit v4 on v3

--- a/solution.py
+++ b/solution.py
@@ -14,7 +14,9 @@
 LANES = 128
 SITE_BLOCK = 64
 QX = 5
-ZY = 16
+Z = 8
+ZY = 2 * Z
+HALF = 32
 GROUP = 28
 CHUNK = 2 * GROUP
 
@@ -37,11 +39,41 @@
     return jnp.take_along_axis(table, index, axis=1)
 
 
-def field_kernel(mom_hbm, table_hbm, noise_hbm, vec_hbm, peer_ref, own_ref, mom_ref, table_ref, noise_ref, vec_ref, phase_re, phase_im, d_ref, sems):
+def combined(mom_ref, phase_re, phase_im, d_ref, out_ref):
+    low = lane_iota(HALF) < SITE_BLOCK
+    for q in range(mom_ref.shape[1]):
+        kind = mom_ref[0, q] + 2
+        re = im = jnp.zeros((HALF, LANES), jnp.float32)
+        for g in range(d_ref.shape[0]):
+            fr = phase_re[q, g : g + 1, :]
+            fi = phase_im[q, g : g + 1, :]
+            dr = d_ref[g, kind, :, 0:LANES]
+            di = d_ref[g, kind, :, LANES:]
+            re = re + (fr * dr - fi * di)
+            im = im + (fr * di + fi * dr)
+        total = jnp.where(low, re, im) + pltpu.roll(jnp.where(low, im, re), SITE_BLOCK, 1)
+        for y in range(2):
+            for b in range(2):
+                r = (y * 2 + b) * Z
+                out_ref[y, pl.ds(b * GROUP + q, Z, stride=CHUNK), :] = total[r : r + Z]
+    for y in range(2):
+        for b in range(2):
+            out_ref[y, pl.ds(b * GROUP + GROUP - 1, Z, stride=CHUNK), :] = jnp.zeros((Z, LANES), jnp.float32)
+
+
+def own_kernel(mom_hbm, phase_re, phase_im, d_ref, out_ref, mom_ref, sem):
+    copy = pltpu.make_async_copy(mom_hbm, mom_ref, sem)
+    copy.start()
+    copy.wait()
+    combined(mom_ref, phase_re, phase_im, d_ref, out_ref)
+
+
+def field_kernel(mom_hbm, table_hbm, noise_hbm, vec_hbm, peer_ref, phase_re, phase_im, own_d, mom_ref, table_ref, noise_ref, vec_ref, peer_d, sems):
     nmom = mom_ref.shape[1]
     steps, spincol, nvec = noise_ref.shape[:3]
     core = lax.axis_index("core")
-    place = (lax.axis_index("z") * 2 + lax.axis_index("yh")) * 2 + core
+    yh = lax.axis_index("yh")
+    place = (lax.axis_index("z") * 2 + yh) * 2 + core
     offset = place * (steps * LANES)
 
     small = [
@@ -77,10 +109,6 @@
         index = jnp.where(index >= 2 * EXTENT, index - 2 * EXTENT, index)
         phase_re[q] = looked_up(cos_table, index)
         phase_im[q] = -looked_up(sin_table, index)
-    zero = jnp.zeros((ZY, LANES), jnp.float32)
-    for out in (peer_ref, own_ref):
-        for b in range(2):
-            out[pl.ds(b * GROUP + GROUP - 1, ZY, stride=CHUNK), :] = zero
 
     one = jnp.bfloat16(1)
     two = jnp.bfloat16(2)
@@ -102,7 +130,8 @@
         for pair in range(spincol // 2):
             rows = []
             for a in (2 * pair, 2 * pair + 1):
-                parts = [noise_ref[step, a, pl.ds(c * 2 + b, ZY, stride=4), :] for c in (1 - core, core) for b in range(2)]
+                firsts = [y * 4 + c * 2 + b for c in (1 - core, core) for y in (1 - yh, yh) for b in range(2)]
+                parts = [noise_ref[step, a, pl.ds(first, Z, stride=8), :] for first in firsts]
                 rows.append(jnp.concatenate(parts, axis=0))
             turned = [pltpu.roll(r, SITE_BLOCK, 1) for r in rows]
             halves = (jnp.where(low64, rows[0], turned[1]), jnp.where(low64, turned[0], rows[1]))
@@ -130,48 +159,53 @@
                 )
                 totals[g] = product if totals[g] is None else totals[g] + product
         for g in range(2):
-            d_ref[step * 2 + g] = totals[g]
-
-    low = lane_iota(nvec) < SITE_BLOCK
-    for q in range(nmom):
-        row = pl.multiple_of((mom_ref[0, q] + 2) * nvec, nvec)
-        re = im = jnp.zeros((nvec, LANES), jnp.float32)
-        for g in range(2 * steps):
-            fr = phase_re[q, g : g + 1, :]
-            fi = phase_im[q, g : g + 1, :]
-            dr = d_ref[g, pl.ds(row, nvec), 0:LANES]
-            di = d_ref[g, pl.ds(row, nvec), LANES:]
-            re = re + (fr * dr - fi * di)
-            im = im + (fr * di + fi * dr)
-        total = jnp.where(low, re, im) + pltpu.roll(jnp.where(low, im, re), SITE_BLOCK, 1)
-        for n, out in enumerate((peer_ref, own_ref)):
-            for b in range(2):
-                r = n * 2 * ZY + b * ZY
-                out[pl.ds(b * GROUP + q, ZY, stride=CHUNK), :] = total[r : r + ZY]
+            for n in range(QX):
+                peer_d[step * 2 + g, n] = totals[g][n * nvec : n * nvec + HALF]
+                own_d[step * 2 + g, n] = totals[g][n * nvec + HALF : (n + 1) * nvec]
+
+    combined(mom_ref, phase_re, phase_im, peer_d, peer_ref)
+
+
+def in_hbm(array):
+    return pltpu.with_memory_space_constraint(array, pltpu.HBM)
 
 
 def partial_fields(momenta, noise, vectors):
     nmom = momenta.shape[1]
     spincol, nvec, sites = noise.shape
     steps = sites // LANES
-    out = pltpu.VMEM((ZY * CHUNK, LANES), jnp.float32)
-    return pl.pallas_call(
+    rows = pltpu.VMEM((2, Z * CHUNK, LANES), jnp.float32)
+    phase = pltpu.VMEM((nmom, 8, LANES), jnp.float32)
+    lines = pltpu.VMEM((2 * steps, QX, HALF, 2 * LANES), jnp.float32)
+    hbm = pl.BlockSpec(memory_space=pltpu.HBM)
+    vmem = pl.BlockSpec(memory_space=pltpu.VMEM)
+    momenta = in_hbm(momenta)
+    peer, *rest = pl.pallas_call(
         field_kernel,
-        in_specs=[pl.BlockSpec(memory_space=pltpu.HBM)] * 4,
-        out_shape=[out, out],
+        in_specs=[hbm] * 4,
+        out_specs=[vmem] * 4,
+        out_shape=[rows, phase, phase, lines],
         scratch_shapes=[
             pltpu.SMEM(momenta.shape, jnp.int32),
             pltpu.VMEM((16, LANES), jnp.float32),
             pltpu.VMEM((steps, spincol, nvec, LANES), jnp.int32),
             pltpu.VMEM((steps, spincol, LANES, LANES), jnp.bfloat16),
-            pltpu.VMEM((nmom, 8, LANES), jnp.float32),
-            pltpu.VMEM((nmom, 8, LANES), jnp.float32),
-            pltpu.VMEM((2 * steps, QX * nvec, 2 * LANES), jnp.float32),
+            lines,
             pltpu.SemaphoreType.DMA((2, steps + 1)),
         ],
         compiler_params=grant(24),
         name="fields",
-    )(*[pltpu.with_memory_space_constraint(a, pltpu.HBM) for a in (momenta, jnp.asarray(trig_table()), noise, vectors)])
+    )(momenta, in_hbm(jnp.asarray(trig_table())), in_hbm(noise), in_hbm(vectors))
+    own = pl.pallas_call(
+        own_kernel,
+        in_specs=[hbm] + [vmem] * 3,
+        out_specs=vmem,
+        out_shape=rows,
+        scratch_shapes=[pltpu.SMEM(momenta.shape, jnp.int32), pltpu.SemaphoreType.DMA],
+        compiler_params=grant(8),
+        name="own",
+    )(momenta, *[pltpu.with_memory_space_constraint(a, pltpu.VMEM) for a in rest])
+    return (peer, own)
 
 
 def mesons_kernel(scale, part_ref, copies_ref, out_ref, row_ref):
@@ -194,7 +228,7 @@
         functools.partial(mesons_kernel, scale),
         out_shape=[
             jax.ShapeDtypeStruct((copies, CHUNK, LANES), jnp.float32),
-            jax.ShapeDtypeStruct((1, 2, nmom, 2, 64), jnp.float32),
+            pltpu.VMEM((1, 2, nmom, 2, 64), jnp.float32),
         ],
         scratch_shapes=[pltpu.VMEM((CHUNK, LANES), jnp.float32)],
         compiler_params=grant(4),
@@ -202,7 +236,9 @@
     )(parts)
 
 
-def traces_kernel(pairs_ref, fields_ref, out_ref):
+def traces_kernel(pairs_ref, mesons_ref, fields_ref, out_ref, mesons_hbm, sem):
+    copy = pltpu.make_async_copy(mesons_ref, mesons_hbm, sem)
+    copy.start()
     lane = lane_iota(CHUNK)
     sign = jnp.where(lane < 64, -1.0, 1.0)
     re = jnp.zeros((CHUNK, LANES), jnp.float32)
@@ -216,17 +252,20 @@
     pad = jnp.zeros((64 - CHUNK, LANES), jnp.float32)
     both = jnp.concatenate([re, pad, im, pad], axis=0)
     out_ref[...] = both.T[0:8, :]
-
-
-def partial_traces(pairs, fields):
-    smem = pl.BlockSpec(memory_space=pltpu.SMEM)
+    copy.wait()
+
+
+def partial_traces(pairs, mesons, fields):
+    vmem = pl.BlockSpec(memory_space=pltpu.VMEM)
     return pl.pallas_call(
         traces_kernel,
-        in_specs=[smem, pl.BlockSpec(memory_space=pltpu.VMEM)],
-        out_shape=jax.ShapeDtypeStruct((8, LANES), jnp.float32),
+        in_specs=[pl.BlockSpec(memory_space=pltpu.SMEM), vmem, vmem],
+        out_specs=[vmem, pl.BlockSpec(memory_space=pltpu.HBM)],
+        out_shape=[pltpu.VMEM((8, LANES), jnp.float32), pltpu.HBM(mesons.shape, jnp.float32)],
+        scratch_shapes=[pltpu.SemaphoreType.DMA],
         compiler_params=grant(4),
         name="traces",
-    )(pairs, fields)
+    )(pairs, mesons, fields)
 
 
 def correlators_kernel(factor, part_ref, out_ref):
@@ -260,10 +299,11 @@
     nmom = momenta.shape[0]
     peer, own = partial_fields(momenta.T, jnp.swapaxes(noise[0], 0, 1), solutions[0])
     arrived = lax.ppermute(peer, "core", [(0, 1), (1, 0)])
-    chunks = (own + arrived).reshape(ZY, CHUNK, LANES)
+    theirs = lax.ppermute(own[0] + arrived[0], "yh", [(0, 1), (1, 0)])
+    chunks = (own[1] + arrived[1] + theirs).reshape(Z, CHUNK, LANES)
     scale = 1.0 / math.sqrt(spincol * sites * 2 * ZY)
-    copies, mesons = summed_mesons(exchange(chunks, ("z", "yh")), scale, lax.axis_size("tm"), nmom)
-    traces = partial_traces(pairs.T, exchange(copies, "tm"))
+    copies, mesons = summed_mesons(exchange(chunks, "z"), scale, lax.axis_size("tm"), nmom)
+    traces, mesons = partial_traces(pairs.T, mesons, exchange(copies, "tm"))
     traces = traces + lax.ppermute(traces, "core", [(0, 1), (1, 0)])
     spread = jnp.broadcast_to(traces, (ZY, *traces.shape))
     correlators = summed_traces(exchange(spread, ("z", "yh")), 1.0 / 64, pairs.shape[0], nmom)

time: 66.8 us -> 67 us (level)
  blocking collectives: 47.1 us -> 39.5 us
  waiting for transfers between devices: 2.27 us -> 8.23 us
  starting transfers between devices: 7.35 us -> 8.73 us
    all_to_all x3, blocking collectives: 47.1 us -> 39.5 us  [exchange(): return lax.all_to_all(array, axis, split_axis=0, concat_axis=0, tiled=True)]
    ppermute x0 -> x1, waiting for transfers between devices: none -> 7.41 us  [local(): theirs = lax.ppermute(own[0] + arrived[0], 'yh', [(0, 1), (1, 0)])]
    ppermute x1, waiting for transfers between devices: 1.44 us -> 0.01 us  [local(): arrived = lax.ppermute(peer, 'core', [(0, 1), (1, 0)])]
    ppermute x0 -> x1, starting transfers between devices: none -> 1.3 us  [local(): theirs = lax.ppermute(own[0] + arrived[0], 'yh', [(0, 1), (1, 0)])]
    pallas_call x2 -> x3, Pallas kernels: 7.57 us -> 8.72 us  [the longest x1 5.42 us: partial_fields(): pl.pallas_call(field_kernel, in_specs=[hbm] * 4, out_specs=[vmem] * 4, ou...]
  transfers between devices with their start and end apart: 2 -> 3, of which waited for: 2 -> 2; matrix products, arithmetic and copies ran while one was open for 0% -> 0% of each run, Pallas kernels for 0% -> 3%
where the time goes in v4:
time: 67 us; the launch traced here: 66.8 us
  blocking collectives  39.5 us (59%)
  Pallas kernels  9.61 us (14%)
  starting transfers between devices  8.73 us (13%)
  waiting for transfers between devices  8.23 us (12%)
  between operations  0.68 us (1%)
    all_to_all x3, blocking collectives, exchange(): return lax.all_to_all(array, axis, split_axis=0, concat_axis=0, tiled=True)  39.5 us
    ppermute x1, waiting for transfers between devices, local(): theirs = lax.ppermute(own[0] + arrived[0], 'yh', [(0, 1), (1, 0)])  7.41 us
    pallas_call x1, Pallas kernels, partial_fields(): pl.pallas_call(field_kernel, in_specs=[hbm] * 4, out_specs=[vmem] * 4, ou...  5.42 us
    ppermute x1, starting transfers between devices, local(): traces = traces + lax.ppermute(traces, 'core', [(0, 1), (1, 0)])  4.14 us
    ppermute x1, starting transfers between devices, local(): arrived = lax.ppermute(peer, 'core', [(0, 1), (1, 0)])  3.28 us
    pallas_call x1, Pallas kernels, partial_fields(): pl.pallas_call(own_kernel, in_specs=[hbm] + [vmem] * 3, out_specs=vmem, o...  1.74 us
    pallas_call x1, Pallas kernels, partial_traces(): pl.pallas_call(traces_kernel, in_specs=[pl.BlockSpec(memory_space=pltpu.S...  1.56 us
  transfers between devices with their start and end apart: 3, of which 2 were waited for; matrix products, arithmetic and copies ran while one was open for 0% of the time, Pallas kernels for 3%

profile of v4, /device:TPU:1, one launch (start us, length us, event | category | flops | bytes accessed | tf_op | source)
XLA Modules:
  0.0 66.8 jit_solution(7752618458099005117)
XLA Ops:
  0.6 5.4 %fields.1 = (f32[2,448,128]{2,1,0:T(8,128)S(1)}, f32[27,8,128]{2,1,0:T(8,128)S(1)}, f32[27,8,128]{2,1,0:T(8,128)S(1)}, f32[8,5,32,256]{3,2,1,0:T(8,128)S(1)}) custom-call(s32[3,27]{1,0:T(4,128)} %bitcast.17, f32[16,128]{1,0:T(8,128)} %constant.2.clone.table_hbm, s32[12,64,512]{2,1,0:T(8,128)} %bitcast.14, bf16[12,512,128]{2,1,0:T(8,128)(2,1)} %bitcast.15), custom_call_target="tpu_custom_call" | custom-call | tf_op jit(solution)/shard_map/fields/pallas_call | solution.py:183
  6.1 3.3 %collective-permute-start = (f32[2,448,128]{2,1,0:T(8,128)S(1)}, f32[2,448,128]{2,1,0:T(8,128)S(1)}, u32[]{:S(2)}, u32[]{:S(2)}) collective-permute-start(f32[2,448,128]{2,1,0:T(8,128)S(1)} %get-tuple-element.13), channel_id=1, source_target_pairs={{0,8},{8,0},{1,9},{9,1},{2,10},{10,2},{3,11},{11,3},{4,12},{12,4},... | collective-permute-start | bytes 1376264 | tf_op jit(solution)/shard_map/ppermute | solution.py:301
  9.3 1.7 %own.1 = f32[2,448,128]{2,1,0:T(8,128)S(1)} custom-call(s32[3,27]{1,0:T(4,128)} %bitcast.18, f32[27,8,128]{2,1,0:T(8,128)S(1)} %get-tuple-element.10.phase_re, f32[27,8,128]{2,1,0:T(8,128)S(1)} %get-tuple-element.11.phase_im, f32[8,5,32,256]{3,2,1,0:T(8,128)S(1)} %get-tuple-element.12.d_ref), custom_call_target="tpu_custom_call" | custom-call | tf_op jit(solution)/shard_map/own/pallas_call | solution.py:199
  11.1 0.0 copy-start
  11.1 0.0 collective-permute-done
  11.1 1.3 %collective-permute-start.1 = (f32[448,128]{1,0:T(8,128)S(1)}, f32[448,128]{1,0:T(8,128)S(1)}, u32[]{:S(2)}, u32[]{:S(2)}) collective-permute-start(f32[448,128]{1,0:T(8,128)S(1)} %fusion), channel_id=1, source_target_pairs={{0,16},{16,0},{1,17},{17,1},{2,18},{18,2},{3,19},{19,3},{4,20},{20... | collective-permute-start | bytes 688136 | tf_op jit(solution)/shard_map/ppermute | solution.py:302
  12.5 7.4 %collective-permute-done.1 = f32[448,128]{1,0:T(8,128)S(1)} collective-permute-done((f32[448,128]{1,0:T(8,128)S(1)}, f32[448,128]{1,0:T(8,128)S(1)}, u32[]{:S(2)}, u32[]{:S(2)}) %collective-permute-start.1) | collective-permute-done | bytes 229408 | tf_op jit(solution)/shard_map/ppermute | solution.py:302
  19.9 15.8 %all_to_all.15.part_ref = f32[8,56,128]{2,1,0:T(8,128)S(1)} all-to-all(f32[8,56,128]{2,1,0:T(8,128)S(1)} %bitcast.16), channel_id=1, replica_groups=mesh['z'=8,'yh'=2,'core'=2,'tm'=8] {'z'}, dimensions={0} | all-to-all | bytes 458752 | tf_op jit(solution)/shard_map/all_to_all | solution.py:294
  35.7 0.1 mesons.1
  35.8 10.5 %all_to_all.16.fields_ref = f32[8,56,128]{2,1,0:T(8,128)S(1)} all-to-all(f32[8,56,128]{2,1,0:T(8,128)S(1)} %get-tuple-element.15), channel_id=1, replica_groups=mesh['z'=8,'yh'=2,'core'=2,'tm'=8] {'tm'}, dimensions={0} | all-to-all | bytes 458752 | tf_op jit(solution)/shard_map/all_to_all | solution.py:294
  46.3 0.0 copy-done
  46.3 1.6 %traces.1 = (f32[8,128]{1,0:T(8,128)S(1)}, f32[1,2,27,2,64]{4,3,2,1,0:T(2,128)}) custom-call(s32[2,8]{1,0:T(2,128)S(1)} %bitcast.13, f32[1,2,27,2,64]{4,3,2,1,0:T(2,128)S(1)} %get-tuple-element.14.mesons_ref, f32[8,56,128]{2,1,0:T(8,128)S(1)} %all_to_all.16.fields_ref), custom_call_target="tpu_custom_call" | custom-call | tf_op jit(solution)/shard_map/traces/pallas_call | solution.py:260
  47.9 4.1 %collective-permute-start.2 = (f32[8,128]{1,0:T(8,128)S(1)}, f32[8,128]{1,0:T(8,128)S(1)}, u32[]{:S(2)}, u32[]{:S(2)}) collective-permute-start(f32[8,128]{1,0:T(8,128)S(1)} %get-tuple-element.17), channel_id=1, source_target_pairs={{0,8},{8,0},{1,9},{9,1},{2,10},{10,2},{3,11},{11,3},{4,12},{12,4},... | collective-permute-start | bytes 12296 | tf_op jit(solution)/shard_map/ppermute | solution.py:307
  52.0 0.8 %collective-permute-done.2 = f32[8,128]{1,0:T(8,128)S(1)} collective-permute-done((f32[8,128]{1,0:T(8,128)S(1)}, f32[8,128]{1,0:T(8,128)S(1)}, u32[]{:S(2)}, u32[]{:S(2)}) %collective-permute-start.2) | collective-permute-done | bytes 4128 | tf_op jit(solution)/shard_map/ppermute | solution.py:307
  52.9 13.2 %all_to_all.17.part_ref = f32[16,8,128]{2,1,0:T(8,128)S(1)} all-to-all(f32[16,8,128]{2,1,0:T(8,128)S(1)} %broadcast_in_dim.3), channel_id=1, replica_groups=mesh['z'=8,'yh'=2,'core'=2,'tm'=8] {'z','yh'}, dimensions={0} | all-to-all | bytes 131072 | tf_op jit(solution)/shard_map/all_to_all | solution.py:294
  66.1 0.8 %correlators.1 = f32[8,2,27]{2,1,0:T(2,128)} custom-call(f32[16,8,128]{2,1,0:T(8,128)S(1)} %all_to_all.17.part_ref), custom_call_target="tpu_custom_call" | custom-call | tf_op jit(solution)/shard_map/correlators/pallas_call | solution.py:285
  (4 shorter events, 0.1 us)
Async XLA Ops:
  6.1 5.0 %collective-permute-start = (f32[2,448,128]{2,1,0:T(8,128)S(1)}, f32[2,448,128]{2,1,0:T(8,128)S(1)}, u32[]{:S(2)}, u32[]{:S(2)}) collective-permute-start(f32[2,448,128]{2,1,0:T(8,128)S(1)} %get-tuple-element.13), channel_id=1, source_target_pairs={{0,8},{8,0},{1,9},{9,1},{2,10},{10,2},{3,11},{11,3},{4,12},{12,4},... | collective-permute-start | bytes 1376264 | tf_op jit(solution)/shard_map/ppermute | solution.py:301
  11.1 35.2 %copy-start = (s32[8,2]{0,1:T(2,128)S(1)}, s32[8,2]{0,1:T(2,128)}, u32[]{:S(2)}) copy-start(s32[8,2]{0,1:T(2,128)} %param.8) | copy-start | bytes 196
  11.1 8.7 %collective-permute-start.1 = (f32[448,128]{1,0:T(8,128)S(1)}, f32[448,128]{1,0:T(8,128)S(1)}, u32[]{:S(2)}, u32[]{:S(2)}) collective-permute-start(f32[448,128]{1,0:T(8,128)S(1)} %fusion), channel_id=1, source_target_pairs={{0,16},{16,0},{1,17},{17,1},{2,18},{18,2},{3,19},{19,3},{4,20},{20... | collective-permute-start | bytes 688136 | tf_op jit(solution)/shard_map/ppermute | solution.py:302
  47.9 5.0 %collective-permute-start.2 = (f32[8,128]{1,0:T(8,128)S(1)}, f32[8,128]{1,0:T(8,128)S(1)}, u32[]{:S(2)}, u32[]{:S(2)}) collective-permute-start(f32[8,128]{1,0:T(8,128)S(1)} %get-tuple-element.17), channel_id=1, source_target_pairs={{0,8},{8,0},{1,9},{9,1},{2,10},{10,2},{3,11},{11,3},{4,12},{12,4},... | collective-permute-start | bytes 12296 | tf_op jit(solution)/shard_map/ppermute | solution.py:307

commit v5 on v4

--- a/solution.py
+++ b/solution.py
@@ -14,11 +14,10 @@
 LANES = 128
 SITE_BLOCK = 64
 QX = 5
-Z = 8
-ZY = 2 * Z
+ZY = 16
 HALF = 32
 GROUP = 28
-CHUNK = 2 * GROUP
+BLOCK = 2 * GROUP
 
 
 def grant(mebibytes):
@@ -40,8 +39,9 @@
 
 
 def combined(mom_ref, phase_re, phase_im, d_ref, out_ref):
+    nmom = mom_ref.shape[1]
     low = lane_iota(HALF) < SITE_BLOCK
-    for q in range(mom_ref.shape[1]):
+    for q in range(nmom):
         kind = mom_ref[0, q] + 2
         re = im = jnp.zeros((HALF, LANES), jnp.float32)
         for g in range(d_ref.shape[0]):
@@ -52,13 +52,10 @@
             re = re + (fr * dr - fi * di)
             im = im + (fr * di + fi * dr)
         total = jnp.where(low, re, im) + pltpu.roll(jnp.where(low, im, re), SITE_BLOCK, 1)
-        for y in range(2):
-            for b in range(2):
-                r = (y * 2 + b) * Z
-                out_ref[y, pl.ds(b * GROUP + q, Z, stride=CHUNK), :] = total[r : r + Z]
-    for y in range(2):
         for b in range(2):
-            out_ref[y, pl.ds(b * GROUP + GROUP - 1, Z, stride=CHUNK), :] = jnp.zeros((Z, LANES), jnp.float32)
+            out_ref[pl.ds(b * GROUP + q, ZY, stride=BLOCK), :] = total[b * ZY : (b + 1) * ZY]
+    for row in range(nmom, BLOCK, GROUP):
+        out_ref[pl.ds(row, ZY, stride=BLOCK), :] = jnp.zeros((ZY, LANES), jnp.float32)
 
 
 def own_kernel(mom_hbm, phase_re, phase_im, d_ref, out_ref, mom_ref, sem):
@@ -72,8 +69,7 @@
     nmom = mom_ref.shape[1]
     steps, spincol, nvec = noise_ref.shape[:3]
     core = lax.axis_index("core")
-    yh = lax.axis_index("yh")
-    place = (lax.axis_index("z") * 2 + yh) * 2 + core
+    place = (lax.axis_index("z") * 2 + lax.axis_index("yh")) * 2 + core
     offset = place * (steps * LANES)
 
     small = [
@@ -130,23 +126,22 @@
         for pair in range(spincol // 2):
             rows = []
             for a in (2 * pair, 2 * pair + 1):
-                firsts = [y * 4 + c * 2 + b for c in (1 - core, core) for y in (1 - yh, yh) for b in range(2)]
-                parts = [noise_ref[step, a, pl.ds(first, Z, stride=8), :] for first in firsts]
+                firsts = [c * 2 + b for c in (1 - core, core) for b in range(2)]
+                parts = [noise_ref[step, a, pl.ds(first, ZY, stride=4), :] for first in firsts]
                 rows.append(jnp.concatenate(parts, axis=0))
             turned = [pltpu.roll(r, SITE_BLOCK, 1) for r in rows]
             halves = (jnp.where(low64, rows[0], turned[1]), jnp.where(low64, turned[0], rows[1]))
             for g in range(2):
                 turns = halves[g].astype(jnp.float32).astype(jnp.bfloat16)
                 er = jnp.abs(turns - two) - one
-                ei = one - jnp.abs(turns - one)
-                left_re = {2: er}
-                left_im = {2: -ei}
+                ei = jnp.abs(turns - one) - one
+                left_re, left_im = ([er], [ei])
                 for k in (1, 2):
                     c, s = waves[g][2 * (k - 1) : 2 * k]
-                    erc, eis, ers, eic = (er * c, ei * s, er * s, ei * c)
-                    left_re[2 + k], left_im[2 + k] = (erc - eis, -(ers + eic))
-                    left_re[2 - k], left_im[2 - k] = (erc + eis, ers - eic)
-                left = [jnp.concatenate([part[n] for n in range(QX)], axis=0) for part in (left_re, left_im)]
+                    minus_s = -s
+                    left_re += [er * c, ei * s]
+                    left_im += [ei * c, er * minus_s]
+                left = [jnp.concatenate(part, axis=0) for part in (left_re, left_im)]
                 re, im = ([], [])
                 for a in (2 * pair, 2 * pair + 1):
                     v = vec_ref[step, a, g * SITE_BLOCK : (g + 1) * SITE_BLOCK, :]
@@ -159,9 +154,13 @@
                 )
                 totals[g] = product if totals[g] is None else totals[g] + product
         for g in range(2):
-            for n in range(QX):
-                peer_d[step * 2 + g, n] = totals[g][n * nvec : n * nvec + HALF]
-                own_d[step * 2 + g, n] = totals[g][n * nvec + HALF : (n + 1) * nvec]
+            for rows, lines in ((slice(0, HALF), peer_d), (slice(HALF, nvec), own_d)):
+                parts = [totals[g][n * nvec : (n + 1) * nvec][rows] for n in range(QX)]
+                at = step * 2 + g
+                lines[at, 2] = parts[0]
+                for k in (1, 2):
+                    lines[at, 2 + k] = parts[2 * k - 1] + parts[2 * k]
+                    lines[at, 2 - k] = parts[2 * k - 1] - parts[2 * k]
 
     combined(mom_ref, phase_re, phase_im, peer_d, peer_ref)
 
@@ -174,7 +173,7 @@
     nmom = momenta.shape[1]
     spincol, nvec, sites = noise.shape
     steps = sites // LANES
-    rows = pltpu.VMEM((2, Z * CHUNK, LANES), jnp.float32)
+    rows = pltpu.VMEM((ZY * BLOCK, LANES), jnp.float32)
     phase = pltpu.VMEM((nmom, 8, LANES), jnp.float32)
     lines = pltpu.VMEM((2 * steps, QX, HALF, 2 * LANES), jnp.float32)
     hbm = pl.BlockSpec(memory_space=pltpu.HBM)
@@ -210,7 +209,7 @@
 
 def mesons_kernel(scale, part_ref, copies_ref, out_ref, row_ref):
     total = part_ref[0]
-    for n in range(1, part_ref.shape[0]):
+    for n in range(1, ZY):
         total = total + part_ref[n]
     total = total * scale
     for n in range(copies_ref.shape[0]):
@@ -227,10 +226,10 @@
     return pl.pallas_call(
         functools.partial(mesons_kernel, scale),
         out_shape=[
-            jax.ShapeDtypeStruct((copies, CHUNK, LANES), jnp.float32),
+            pltpu.VMEM((copies, BLOCK, LANES), jnp.float32),
             pltpu.VMEM((1, 2, nmom, 2, 64), jnp.float32),
         ],
-        scratch_shapes=[pltpu.VMEM((CHUNK, LANES), jnp.float32)],
+        scratch_shapes=[pltpu.VMEM((BLOCK, LANES), jnp.float32)],
         compiler_params=grant(4),
         name="mesons",
     )(parts)
@@ -239,9 +238,9 @@
 def traces_kernel(pairs_ref, mesons_ref, fields_ref, out_ref, mesons_hbm, sem):
     copy = pltpu.make_async_copy(mesons_ref, mesons_hbm, sem)
     copy.start()
-    lane = lane_iota(CHUNK)
+    lane = lane_iota(BLOCK)
     sign = jnp.where(lane < 64, -1.0, 1.0)
-    re = jnp.zeros((CHUNK, LANES), jnp.float32)
+    re = jnp.zeros((BLOCK, LANES), jnp.float32)
     im = re
     for k in range(pairs_ref.shape[1]):
         source = fields_ref[pairs_ref[0, k]]
@@ -249,9 +248,11 @@
         swapped = pltpu.roll(source, 64, 1) * sign
         re = jnp.where(lane == k, jnp.sum(sink * source, axis=1, keepdims=True), re)
         im = jnp.where(lane == k, jnp.sum(sink * swapped, axis=1, keepdims=True), im)
-    pad = jnp.zeros((64 - CHUNK, LANES), jnp.float32)
-    both = jnp.concatenate([re, pad, im, pad], axis=0)
-    out_ref[...] = both.T[0:8, :]
+    re = re[0:32] + pltpu.roll(re, BLOCK - GROUP, 0)[0:32]
+    im = im[0:32] + pltpu.roll(im, BLOCK - GROUP, 0)[0:32]
+    pad = jnp.zeros((64, LANES), jnp.float32)
+    both = jnp.concatenate([re, im, pad], axis=0).T
+    out_ref[...] = both[0:4] + pltpu.roll(both, 64, 1)[4:8]
     copy.wait()
 
 
@@ -261,7 +262,7 @@
         traces_kernel,
         in_specs=[pl.BlockSpec(memory_space=pltpu.SMEM), vmem, vmem],
         out_specs=[vmem, pl.BlockSpec(memory_space=pltpu.HBM)],
-        out_shape=[pltpu.VMEM((8, LANES), jnp.float32), pltpu.HBM(mesons.shape, jnp.float32)],
+        out_shape=[pltpu.VMEM((4, LANES), jnp.float32), pltpu.HBM(mesons.shape, jnp.float32)],
         scratch_shapes=[pltpu.SemaphoreType.DMA],
         compiler_params=grant(4),
         name="traces",
@@ -274,11 +275,11 @@
         total = total + part_ref[n]
     total = total * factor
     nmom = out_ref.shape[2]
-    total = total + pltpu.roll(total, LANES - GROUP, 1)
-    moved = pltpu.roll(total, 64, 1)
     for k in range(out_ref.shape[0]):
-        out_ref[k, 0:1, :] = total[k : k + 1, 0:nmom]
-        out_ref[k, 1:2, :] = moved[k : k + 1, 0:nmom]
+        for c in range(2):
+            first = (k // 4) * 64 + c * 32
+            moved = total if first == 0 else pltpu.roll(total, LANES - first, 1)
+            out_ref[k, c : c + 1, :] = moved[k % 4 : k % 4 + 1, 0:nmom]
 
 
 def summed_traces(parts, factor, npairs, nmom):
@@ -299,10 +300,8 @@
     nmom = momenta.shape[0]
     peer, own = partial_fields(momenta.T, jnp.swapaxes(noise[0], 0, 1), solutions[0])
     arrived = lax.ppermute(peer, "core", [(0, 1), (1, 0)])
-    theirs = lax.ppermute(own[0] + arrived[0], "yh", [(0, 1), (1, 0)])
-    chunks = (own[1] + arrived[1] + theirs).reshape(Z, CHUNK, LANES)
     scale = 1.0 / math.sqrt(spincol * sites * 2 * ZY)
-    copies, mesons = summed_mesons(exchange(chunks, "z"), scale, lax.axis_size("tm"), nmom)
+    copies, mesons = summed_mesons(exchange((own + arrived).reshape(ZY, BLOCK, LANES), ("z", "yh")), scale, lax.axis_size("tm"), nmom)
     traces, mesons = partial_traces(pairs.T, mesons, exchange(copies, "tm"))
     traces = traces + lax.ppermute(traces, "core", [(0, 1), (1, 0)])
     spread = jnp.broadcast_to(traces, (ZY, *traces.shape))

time: 67 us -> 65.6 us (0.979)
  blocking collectives: 39.5 us -> 47.2 us
  waiting for transfers between devices: 8.23 us -> 0.82 us
  starting transfers between devices: 8.73 us -> 7.08 us
    all_to_all x3, blocking collectives: 39.5 us -> 47.2 us  [exchange(): return lax.all_to_all(array, axis, split_axis=0, concat_axis=0, tiled=True)]
    ppermute x1 -> x0, waiting for transfers between devices: 7.41 us -> none  [local(): theirs = lax.ppermute(own[0] + arrived[0], 'yh', [(0, 1), (1, 0)])]
    ppermute x1 -> x0, starting transfers between devices: 1.3 us -> none  [local(): theirs = lax.ppermute(own[0] + arrived[0], 'yh', [(0, 1), (1, 0)])]
  transfers between devices with their start and end apart: 3 -> 2, of which waited for: 2 -> 1; matrix products, arithmetic and copies ran while one was open for 0% -> 0% of each run, Pallas kernels for 3% -> 3%
where the time goes in v5:
time: 65.6 us; the launch traced here: 65.4 us
  blocking collectives  47.2 us (72%)
  Pallas kernels  9.49 us (14%)
  starting transfers between devices  7.08 us (11%)
  waiting for transfers between devices  0.82 us (1%)
  between operations  0.68 us (1%)
    all_to_all x3, blocking collectives, exchange(): return lax.all_to_all(array, axis, split_axis=0, concat_axis=0, tiled=True)  47.2 us
    pallas_call x1, Pallas kernels, partial_fields(): pl.pallas_call(field_kernel, in_specs=[hbm] * 4, out_specs=[vmem] * 4, ou...  5.35 us
    ppermute x1, starting transfers between devices, local(): traces = traces + lax.ppermute(traces, 'core', [(0, 1), (1, 0)])  3.8 us
    ppermute x1, starting transfers between devices, local(): arrived = lax.ppermute(peer, 'core', [(0, 1), (1, 0)])  3.29 us
    pallas_call x1, Pallas kernels, partial_fields(): pl.pallas_call(own_kernel, in_specs=[hbm] + [vmem] * 3, out_specs=vmem, o...  1.74 us
    pallas_call x1, Pallas kernels, partial_traces(): pl.pallas_call(traces_kernel, in_specs=[pl.BlockSpec(memory_space=pltpu.S...  1.56 us
  transfers between devices with their start and end apart: 2, of which 1 were waited for; matrix products, arithmetic and copies ran while one was open for 0% of the time, Pallas kernels for 3%

profile of v5, /device:TPU:1, one launch (start us, length us, event | category | flops | bytes accessed | tf_op | source)
XLA Modules:
  0.0 65.4 jit_solution(621378064692690252)
XLA Ops:
  0.6 5.3 %fields.1 = (f32[896,128]{1,0:T(8,128)S(1)}, f32[27,8,128]{2,1,0:T(8,128)S(1)}, f32[27,8,128]{2,1,0:T(8,128)S(1)}, f32[8,5,32,256]{3,2,1,0:T(8,128)S(1)}) custom-call(s32[3,27]{1,0:T(4,128)} %bitcast.11, f32[16,128]{1,0:T(8,128)} %constant.2.clone.table_hbm, s32[12,64,512]{2,1,0:T(8,128)} %bitcast.9, bf16[12,512,128]{2,1,0:T(8,128)(2,1)} %bitcast.10), custom_call_target="tpu_custom_call" | custom-call | tf_op jit(solution)/shard_map/fields/pallas_call | solution.py:182
  6.0 3.3 %collective-permute-start = (f32[896,128]{1,0:T(8,128)S(1)}, f32[896,128]{1,0:T(8,128)S(1)}, u32[]{:S(2)}, u32[]{:S(2)}) collective-permute-start(f32[896,128]{1,0:T(8,128)S(1)} %get-tuple-element.13), channel_id=1, source_target_pairs={{0,8},{8,0},{1,9},{9,1},{2,10},{10,2},{3,11},{11,3},{4,12},{12,4},... | collective-permute-start | bytes 1376264 | tf_op jit(solution)/shard_map/ppermute | solution.py:302
  9.3 1.7 %own.1 = f32[896,128]{1,0:T(8,128)S(1)} custom-call(s32[3,27]{1,0:T(4,128)} %bitcast.12, f32[27,8,128]{2,1,0:T(8,128)S(1)} %get-tuple-element.10.phase_re, f32[27,8,128]{2,1,0:T(8,128)S(1)} %get-tuple-element.11.phase_im, f32[8,5,32,256]{3,2,1,0:T(8,128)S(1)} %get-tuple-element.12.d_ref), custom_call_target="tpu_custom_call" | custom-call | tf_op jit(solution)/shard_map/own/pallas_call | solution.py:198
  11.0 0.0 copy-start
  11.0 0.0 collective-permute-done
  11.0 0.1 add.6
  11.1 25.5 %all_to_all.15.part_ref = f32[16,56,128]{2,1,0:T(8,128)S(1)} all-to-all(f32[16,56,128]{2,1,0:T(8,128)S(1)} %bitcast.8), channel_id=1, replica_groups=mesh['z'=8,'yh'=2,'core'=2,'tm'=8] {'z','yh'}, dimensions={0} | all-to-all | bytes 917504 | tf_op jit(solution)/shard_map/all_to_all | solution.py:295
  36.7 0.2 mesons.1
  36.8 9.6 %all_to_all.16.fields_ref = f32[8,56,128]{2,1,0:T(8,128)S(1)} all-to-all(f32[8,56,128]{2,1,0:T(8,128)S(1)} %get-tuple-element.15), channel_id=1, replica_groups=mesh['z'=8,'yh'=2,'core'=2,'tm'=8] {'tm'}, dimensions={0} | all-to-all | bytes 458752 | tf_op jit(solution)/shard_map/all_to_all | solution.py:295
  46.4 0.0 copy-done
  46.4 1.6 %traces.1 = (f32[4,128]{1,0:T(4,128)S(1)}, f32[1,2,27,2,64]{4,3,2,1,0:T(2,128)}) custom-call(s32[2,8]{1,0:T(2,128)S(1)} %bitcast.7, f32[1,2,27,2,64]{4,3,2,1,0:T(2,128)S(1)} %get-tuple-element.14.mesons_ref, f32[8,56,128]{2,1,0:T(8,128)S(1)} %all_to_all.16.fields_ref), custom_call_target="tpu_custom_call" | custom-call | tf_op jit(solution)/shard_map/traces/pallas_call | solution.py:261
  48.0 3.8 %collective-permute-start.1 = (f32[4,128]{1,0:T(4,128)S(1)}, f32[4,128]{1,0:T(4,128)S(1)}, u32[]{:S(2)}, u32[]{:S(2)}) collective-permute-start(f32[4,128]{1,0:T(4,128)S(1)} %get-tuple-element.17), channel_id=1, source_target_pairs={{0,8},{8,0},{1,9},{9,1},{2,10},{10,2},{3,11},{11,3},{4,12},{12,4},... | collective-permute-start | bytes 6152 | tf_op jit(solution)/shard_map/ppermute | solution.py:306
  51.8 0.8 %collective-permute-done.1 = f32[4,128]{1,0:T(4,128)S(1)} collective-permute-done((f32[4,128]{1,0:T(4,128)S(1)}, f32[4,128]{1,0:T(4,128)S(1)}, u32[]{:S(2)}, u32[]{:S(2)}) %collective-permute-start.1) | collective-permute-done | bytes 2080 | tf_op jit(solution)/shard_map/ppermute | solution.py:306
  52.6 12.1 %all_to_all.17.part_ref = f32[16,4,128]{2,1,0:T(4,128)S(1)} all-to-all(f32[16,4,128]{2,1,0:T(4,128)S(1)} %broadcast_in_dim.3), channel_id=1, replica_groups=mesh['z'=8,'yh'=2,'core'=2,'tm'=8] {'z','yh'}, dimensions={0} | all-to-all | bytes 65536 | tf_op jit(solution)/shard_map/all_to_all | solution.py:295
  64.7 0.7 %correlators.1 = f32[8,2,27]{2,1,0:T(2,128)} custom-call(f32[16,4,128]{2,1,0:T(4,128)S(1)} %all_to_all.17.part_ref), custom_call_target="tpu_custom_call" | custom-call | tf_op jit(solution)/shard_map/correlators/pallas_call | solution.py:286
  (2 shorter events, 0.0 us)
Async XLA Ops:
  6.0 5.1 %collective-permute-start = (f32[896,128]{1,0:T(8,128)S(1)}, f32[896,128]{1,0:T(8,128)S(1)}, u32[]{:S(2)}, u32[]{:S(2)}) collective-permute-start(f32[896,128]{1,0:T(8,128)S(1)} %get-tuple-element.13), channel_id=1, source_target_pairs={{0,8},{8,0},{1,9},{9,1},{2,10},{10,2},{3,11},{11,3},{4,12},{12,4},... | collective-permute-start | bytes 1376264 | tf_op jit(solution)/shard_map/ppermute | solution.py:302
  11.0 35.4 %copy-start = (s32[8,2]{0,1:T(2,128)S(1)}, s32[8,2]{0,1:T(2,128)}, u32[]{:S(2)}) copy-start(s32[8,2]{0,1:T(2,128)} %param.8) | copy-start | bytes 196
  48.0 4.6 %collective-permute-start.1 = (f32[4,128]{1,0:T(4,128)S(1)}, f32[4,128]{1,0:T(4,128)S(1)}, u32[]{:S(2)}, u32[]{:S(2)}) collective-permute-start(f32[4,128]{1,0:T(4,128)S(1)} %get-tuple-element.17), channel_id=1, source_target_pairs={{0,8},{8,0},{1,9},{9,1},{2,10},{10,2},{3,11},{11,3},{4,12},{12,4},... | collective-permute-start | bytes 6152 | tf_op jit(solution)/shard_map/ppermute | solution.py:306

commit v6 on v5

--- a/solution.py
+++ b/solution.py
@@ -18,6 +18,7 @@
 HALF = 32
 GROUP = 28
 BLOCK = 2 * GROUP
+FACTORS = (1.624205, 1.13242)
 
 
 def grant(mebibytes):
@@ -38,34 +39,42 @@
     return jnp.take_along_axis(table, index, axis=1)
 
 
-def combined(mom_ref, phase_re, phase_im, d_ref, out_ref):
+def combined(mom_ref, phase_re, phase_im, lines, first_block, out_ref, sums_ref=None, last=True, part=None):
     nmom = mom_ref.shape[1]
     low = lane_iota(HALF) < SITE_BLOCK
-    for q in range(nmom):
+    for q in range(*(part or (0, nmom))):
         kind = mom_ref[0, q] + 2
-        re = im = jnp.zeros((HALF, LANES), jnp.float32)
-        for g in range(d_ref.shape[0]):
-            fr = phase_re[q, g : g + 1, :]
-            fi = phase_im[q, g : g + 1, :]
-            dr = d_ref[g, kind, :, 0:LANES]
-            di = d_ref[g, kind, :, LANES:]
+        if first_block == 0:
+            re = im = jnp.zeros((HALF, LANES), jnp.float32)
+        else:
+            re, im = (sums_ref[q, 0], sums_ref[q, 1])
+        for g in range(lines.shape[0]):
+            fr = phase_re[q, first_block + g : first_block + g + 1, :]
+            fi = phase_im[q, first_block + g : first_block + g + 1, :]
+            dr = lines[g, kind, :, 0:LANES]
+            di = lines[g, kind, :, LANES:]
             re = re + (fr * dr - fi * di)
             im = im + (fr * di + fi * dr)
+        if not last:
+            sums_ref[q, 0] = re
+            sums_ref[q, 1] = im
+            continue
         total = jnp.where(low, re, im) + pltpu.roll(jnp.where(low, im, re), SITE_BLOCK, 1)
         for b in range(2):
             out_ref[pl.ds(b * GROUP + q, ZY, stride=BLOCK), :] = total[b * ZY : (b + 1) * ZY]
-    for row in range(nmom, BLOCK, GROUP):
-        out_ref[pl.ds(row, ZY, stride=BLOCK), :] = jnp.zeros((ZY, LANES), jnp.float32)
+    if last:
+        for row in range(nmom, BLOCK, GROUP):
+            out_ref[pl.ds(row, ZY, stride=BLOCK), :] = jnp.zeros((ZY, LANES), jnp.float32)
 
 
 def own_kernel(mom_hbm, phase_re, phase_im, d_ref, out_ref, mom_ref, sem):
     copy = pltpu.make_async_copy(mom_hbm, mom_ref, sem)
     copy.start()
     copy.wait()
-    combined(mom_ref, phase_re, phase_im, d_ref, out_ref)
-
-
-def field_kernel(mom_hbm, table_hbm, noise_hbm, vec_hbm, peer_ref, phase_re, phase_im, own_d, mom_ref, table_ref, noise_ref, vec_ref, peer_d, sems):
+    combined(mom_ref, phase_re, phase_im, d_ref, 0, out_ref)
+
+
+def field_kernel(mom_hbm, table_hbm, noise_hbm, vec_hbm, peer_ref, phase_re, phase_im, own_d, mom_ref, table_ref, noise_ref, vec_ref, even_d, odd_d, sums_ref, sems):
     nmom = mom_ref.shape[1]
     steps, spincol, nvec = noise_ref.shape[:3]
     core = lax.axis_index("core")
@@ -103,8 +112,10 @@
         index = mom_ref[1, q] * y + mom_ref[2, q] * z
         index = jnp.where(index < 0, index + 3 * EXTENT, index)
         index = jnp.where(index >= 2 * EXTENT, index - 2 * EXTENT, index)
-        phase_re[q] = looked_up(cos_table, index)
-        phase_im[q] = -looked_up(sin_table, index)
+        kind = jnp.abs(mom_ref[0, q])
+        undo = jnp.where(kind == 0, 1.0, jnp.where(kind == 1, 1.0 / FACTORS[0], 1.0 / FACTORS[1]))
+        phase_re[q] = looked_up(cos_table, index) * undo
+        phase_im[q] = -looked_up(sin_table, index) * undo
 
     one = jnp.bfloat16(1)
     two = jnp.bfloat16(2)
@@ -117,13 +128,24 @@
             x = jnp.where(x >= EXTENT, x - EXTENT, x)
             x2 = 2 * x
             x2 = jnp.where(x2 >= EXTENT, x2 - EXTENT, x2)
-            waves.append([looked_up(t, i)[0:1, :].astype(jnp.bfloat16) for i in (x, x2) for t in (cos_table, sin_table)])
+            waves.append(
+                [
+                    (looked_up(t, i)[0:1, :] * f).astype(jnp.bfloat16)
+                    for i, f in zip((x, x2), FACTORS, strict=True)
+                    for t in (cos_table, sin_table)
+                ]
+            )
             masks.append(jnp.where((site < EXTENT - into) == low64, 1.0, 0.0).astype(jnp.bfloat16))
-        for copy in blocks[step]:
+        for copy in [] if step > 1 else blocks[0] if step == 0 else sum(blocks[1:], []):
             copy.wait()
+        lines, before = (odd_d, even_d) if step % 2 else (even_d, odd_d)
 
         totals = [None, None]
+        each = -(-nmom // (spincol // 2))
         for pair in range(spincol // 2):
+            if step > 0:
+                part = (pair * each, min(nmom, (pair + 1) * each))
+                combined(mom_ref, phase_re, phase_im, before, 2 * step - 2, peer_ref, sums_ref, last=False, part=part)
             rows = []
             for a in (2 * pair, 2 * pair + 1):
                 firsts = [c * 2 + b for c in (1 - core, core) for b in range(2)]
@@ -154,15 +176,16 @@
                 )
                 totals[g] = product if totals[g] is None else totals[g] + product
         for g in range(2):
-            for rows, lines in ((slice(0, HALF), peer_d), (slice(HALF, nvec), own_d)):
-                parts = [totals[g][n * nvec : (n + 1) * nvec][rows] for n in range(QX)]
-                at = step * 2 + g
-                lines[at, 2] = parts[0]
-                for k in (1, 2):
-                    lines[at, 2 + k] = parts[2 * k - 1] + parts[2 * k]
-                    lines[at, 2 - k] = parts[2 * k - 1] - parts[2 * k]
-
-    combined(mom_ref, phase_re, phase_im, peer_d, peer_ref)
+            parts = [totals[g][n * nvec : (n + 1) * nvec] for n in range(QX)]
+            values = {2: parts[0]}
+            for k in (1, 2):
+                values[2 + k] = parts[2 * k - 1] + parts[2 * k]
+                values[2 - k] = parts[2 * k - 1] - parts[2 * k]
+            for n in range(QX):
+                lines[g, n] = values[n][:HALF]
+                own_d[step * 2 + g, n] = values[n][HALF:]
+
+    combined(mom_ref, phase_re, phase_im, lines, 2 * steps - 2, peer_ref, sums_ref)
 
 
 def in_hbm(array):
@@ -189,7 +212,9 @@
             pltpu.VMEM((16, LANES), jnp.float32),
             pltpu.VMEM((steps, spincol, nvec, LANES), jnp.int32),
             pltpu.VMEM((steps, spincol, LANES, LANES), jnp.bfloat16),
-            lines,
+            pltpu.VMEM((2, QX, HALF, 2 * LANES), jnp.float32),
+            pltpu.VMEM((2, QX, HALF, 2 * LANES), jnp.float32),
+            pltpu.VMEM((nmom, 2, HALF, LANES), jnp.float32),
             pltpu.SemaphoreType.DMA((2, steps + 1)),
         ],
         compiler_params=grant(24),

time: 65.6 us -> 65 us (level)
  no operation moved by 1% of the time
where the time goes in v6:
time: 65 us; the launch traced here: 64.8 us
  blocking collectives  47.2 us (73%)
  Pallas kernels  8.92 us (14%)
  starting transfers between devices  7.07 us (11%)
  waiting for transfers between devices  0.82 us (1%)
  between operations  0.68 us (1%)
    all_to_all x3, blocking collectives, exchange(): return lax.all_to_all(array, axis, split_axis=0, concat_axis=0, tiled=True)  47.2 us
    pallas_call x1, Pallas kernels, partial_fields(): pl.pallas_call(field_kernel, in_specs=[hbm] * 4, out_specs=[vmem] * 4, ou...  4.78 us
    ppermute x1, starting transfers between devices, local(): traces = traces + lax.ppermute(traces, 'core', [(0, 1), (1, 0)])  3.8 us
    ppermute x1, starting transfers between devices, local(): arrived = lax.ppermute(peer, 'core', [(0, 1), (1, 0)])  3.28 us
    pallas_call x1, Pallas kernels, partial_fields(): pl.pallas_call(own_kernel, in_specs=[hbm] + [vmem] * 3, out_specs=vmem, o...  1.74 us
    pallas_call x1, Pallas kernels, partial_traces(): pl.pallas_call(traces_kernel, in_specs=[pl.BlockSpec(memory_space=pltpu.S...  1.56 us
  transfers between devices with their start and end apart: 2, of which 1 were waited for; matrix products, arithmetic and copies ran while one was open for 0% of the time, Pallas kernels for 3%

profile of v6, /device:TPU:1, one launch (start us, length us, event | category | flops | bytes accessed | tf_op | source)
XLA Modules:
  0.0 64.8 jit_solution(518113268786422264)
XLA Ops:
  0.6 4.8 %fields.1 = (f32[896,128]{1,0:T(8,128)S(1)}, f32[27,8,128]{2,1,0:T(8,128)S(1)}, f32[27,8,128]{2,1,0:T(8,128)S(1)}, f32[8,5,32,256]{3,2,1,0:T(8,128)S(1)}) custom-call(s32[3,27]{1,0:T(4,128)} %bitcast.11, f32[16,128]{1,0:T(8,128)} %constant.2.clone.table_hbm, s32[12,64,512]{2,1,0:T(8,128)} %bitcast.9, bf16[12,512,128]{2,1,0:T(8,128)(2,1)} %bitcast.10), custom_call_target="tpu_custom_call" | custom-call | tf_op jit(solution)/shard_map/fields/pallas_call | solution.py:205
  5.4 3.3 %collective-permute-start = (f32[896,128]{1,0:T(8,128)S(1)}, f32[896,128]{1,0:T(8,128)S(1)}, u32[]{:S(2)}, u32[]{:S(2)}) collective-permute-start(f32[896,128]{1,0:T(8,128)S(1)} %get-tuple-element.13), channel_id=1, source_target_pairs={{0,8},{8,0},{1,9},{9,1},{2,10},{10,2},{3,11},{11,3},{4,12},{12,4},... | collective-permute-start | bytes 1376264 | tf_op jit(solution)/shard_map/ppermute | solution.py:327
  8.7 1.7 %own.1 = f32[896,128]{1,0:T(8,128)S(1)} custom-call(s32[3,27]{1,0:T(4,128)} %bitcast.12, f32[27,8,128]{2,1,0:T(8,128)S(1)} %get-tuple-element.10.phase_re, f32[27,8,128]{2,1,0:T(8,128)S(1)} %get-tuple-element.11.phase_im, f32[8,5,32,256]{3,2,1,0:T(8,128)S(1)} %get-tuple-element.12.d_ref), custom_call_target="tpu_custom_call" | custom-call | tf_op jit(solution)/shard_map/own/pallas_call | solution.py:223
  10.4 0.0 copy-start
  10.5 0.0 collective-permute-done
  10.5 0.1 add.6
  10.5 25.6 %all_to_all.15.part_ref = f32[16,56,128]{2,1,0:T(8,128)S(1)} all-to-all(f32[16,56,128]{2,1,0:T(8,128)S(1)} %bitcast.8), channel_id=1, replica_groups=mesh['z'=8,'yh'=2,'core'=2,'tm'=8] {'z','yh'}, dimensions={0} | all-to-all | bytes 917504 | tf_op jit(solution)/shard_map/all_to_all | solution.py:320
  36.1 0.2 mesons.1
  36.2 9.6 %all_to_all.16.fields_ref = f32[8,56,128]{2,1,0:T(8,128)S(1)} all-to-all(f32[8,56,128]{2,1,0:T(8,128)S(1)} %get-tuple-element.15), channel_id=1, replica_groups=mesh['z'=8,'yh'=2,'core'=2,'tm'=8] {'tm'}, dimensions={0} | all-to-all | bytes 458752 | tf_op jit(solution)/shard_map/all_to_all | solution.py:320
  45.8 0.0 copy-done
  45.8 1.6 %traces.1 = (f32[4,128]{1,0:T(4,128)S(1)}, f32[1,2,27,2,64]{4,3,2,1,0:T(2,128)}) custom-call(s32[2,8]{1,0:T(2,128)S(1)} %bitcast.7, f32[1,2,27,2,64]{4,3,2,1,0:T(2,128)S(1)} %get-tuple-element.14.mesons_ref, f32[8,56,128]{2,1,0:T(8,128)S(1)} %all_to_all.16.fields_ref), custom_call_target="tpu_custom_call" | custom-call | tf_op jit(solution)/shard_map/traces/pallas_call | solution.py:286
  47.4 3.8 %collective-permute-start.1 = (f32[4,128]{1,0:T(4,128)S(1)}, f32[4,128]{1,0:T(4,128)S(1)}, u32[]{:S(2)}, u32[]{:S(2)}) collective-permute-start(f32[4,128]{1,0:T(4,128)S(1)} %get-tuple-element.17), channel_id=1, source_target_pairs={{0,8},{8,0},{1,9},{9,1},{2,10},{10,2},{3,11},{11,3},{4,12},{12,4},... | collective-permute-start | bytes 6152 | tf_op jit(solution)/shard_map/ppermute | solution.py:331
  51.2 0.8 %collective-permute-done.1 = f32[4,128]{1,0:T(4,128)S(1)} collective-permute-done((f32[4,128]{1,0:T(4,128)S(1)}, f32[4,128]{1,0:T(4,128)S(1)}, u32[]{:S(2)}, u32[]{:S(2)}) %collective-permute-start.1) | collective-permute-done | bytes 2080 | tf_op jit(solution)/shard_map/ppermute | solution.py:331
  52.0 12.1 %all_to_all.17.part_ref = f32[16,4,128]{2,1,0:T(4,128)S(1)} all-to-all(f32[16,4,128]{2,1,0:T(4,128)S(1)} %broadcast_in_dim.3), channel_id=1, replica_groups=mesh['z'=8,'yh'=2,'core'=2,'tm'=8] {'z','yh'}, dimensions={0} | all-to-all | bytes 65536 | tf_op jit(solution)/shard_map/all_to_all | solution.py:320
  64.1 0.7 %correlators.1 = f32[8,2,27]{2,1,0:T(2,128)} custom-call(f32[16,4,128]{2,1,0:T(4,128)S(1)} %all_to_all.17.part_ref), custom_call_target="tpu_custom_call" | custom-call | tf_op jit(solution)/shard_map/correlators/pallas_call | solution.py:311
  (2 shorter events, 0.0 us)
Async XLA Ops:
  5.4 5.0 %collective-permute-start = (f32[896,128]{1,0:T(8,128)S(1)}, f32[896,128]{1,0:T(8,128)S(1)}, u32[]{:S(2)}, u32[]{:S(2)}) collective-permute-start(f32[896,128]{1,0:T(8,128)S(1)} %get-tuple-element.13), channel_id=1, source_target_pairs={{0,8},{8,0},{1,9},{9,1},{2,10},{10,2},{3,11},{11,3},{4,12},{12,4},... | collective-permute-start | bytes 1376264 | tf_op jit(solution)/shard_map/ppermute | solution.py:327
  10.4 35.4 %copy-start = (s32[8,2]{0,1:T(2,128)S(1)}, s32[8,2]{0,1:T(2,128)}, u32[]{:S(2)}) copy-start(s32[8,2]{0,1:T(2,128)} %param.8) | copy-start | bytes 196
  47.4 4.6 %collective-permute-start.1 = (f32[4,128]{1,0:T(4,128)S(1)}, f32[4,128]{1,0:T(4,128)S(1)}, u32[]{:S(2)}, u32[]{:S(2)}) collective-permute-start(f32[4,128]{1,0:T(4,128)S(1)} %get-tuple-element.17), channel_id=1, source_target_pairs={{0,8},{8,0},{1,9},{9,1},{2,10},{10,2},{3,11},{11,3},{4,12},{12,4},... | collective-permute-start | bytes 6152 | tf_op jit(solution)/shard_map/ppermute | solution.py:331

commit v7 on v6

--- a/solution.py
+++ b/solution.py
@@ -67,11 +67,8 @@
             out_ref[pl.ds(row, ZY, stride=BLOCK), :] = jnp.zeros((ZY, LANES), jnp.float32)
 
 
-def own_kernel(mom_hbm, phase_re, phase_im, d_ref, out_ref, mom_ref, sem):
-    copy = pltpu.make_async_copy(mom_hbm, mom_ref, sem)
-    copy.start()
-    copy.wait()
-    combined(mom_ref, phase_re, phase_im, d_ref, 0, out_ref)
+def own_kernel(mom_ref, phase_re, phase_im, d_ref, out_ref):
+    combined(mom_ref[...], phase_re, phase_im, d_ref, 0, out_ref)
 
 
 def field_kernel(mom_hbm, table_hbm, noise_hbm, vec_hbm, peer_ref, phase_re, phase_im, own_d, mom_ref, table_ref, noise_ref, vec_ref, even_d, odd_d, sums_ref, sems):
@@ -201,7 +198,6 @@
     lines = pltpu.VMEM((2 * steps, QX, HALF, 2 * LANES), jnp.float32)
     hbm = pl.BlockSpec(memory_space=pltpu.HBM)
     vmem = pl.BlockSpec(memory_space=pltpu.VMEM)
-    momenta = in_hbm(momenta)
     peer, *rest = pl.pallas_call(
         field_kernel,
         in_specs=[hbm] * 4,
@@ -219,16 +215,15 @@
         ],
         compiler_params=grant(24),
         name="fields",
-    )(momenta, in_hbm(jnp.asarray(trig_table())), in_hbm(noise), in_hbm(vectors))
+    )(in_hbm(momenta), in_hbm(jnp.asarray(trig_table())), in_hbm(noise), in_hbm(vectors))
     own = pl.pallas_call(
         own_kernel,
-        in_specs=[hbm] + [vmem] * 3,
+        in_specs=[vmem] * 4,
         out_specs=vmem,
         out_shape=rows,
-        scratch_shapes=[pltpu.SMEM(momenta.shape, jnp.int32), pltpu.SemaphoreType.DMA],
         compiler_params=grant(8),
         name="own",
-    )(momenta, *[pltpu.with_memory_space_constraint(a, pltpu.VMEM) for a in rest])
+    )(*[pltpu.with_memory_space_constraint(a, pltpu.VMEM) for a in (momenta, *rest)])
     return (peer, own)
 
 
@@ -267,9 +262,10 @@
     sign = jnp.where(lane < 64, -1.0, 1.0)
     re = jnp.zeros((BLOCK, LANES), jnp.float32)
     im = re
+    pairs = pairs_ref[...]
     for k in range(pairs_ref.shape[1]):
-        source = fields_ref[pairs_ref[0, k]]
-        sink = fields_ref[pairs_ref[1, k]]
+        source = fields_ref[pairs[0, k]]
+        sink = fields_ref[pairs[1, k]]
         swapped = pltpu.roll(source, 64, 1) * sign
         re = jnp.where(lane == k, jnp.sum(sink * source, axis=1, keepdims=True), re)
         im = jnp.where(lane == k, jnp.sum(sink * swapped, axis=1, keepdims=True), im)
@@ -285,7 +281,7 @@
     vmem = pl.BlockSpec(memory_space=pltpu.VMEM)
     return pl.pallas_call(
         traces_kernel,
-        in_specs=[pl.BlockSpec(memory_space=pltpu.SMEM), vmem, vmem],
+        in_specs=[vmem, vmem, vmem],
         out_specs=[vmem, pl.BlockSpec(memory_space=pltpu.HBM)],
         out_shape=[pltpu.VMEM((4, LANES), jnp.float32), pltpu.HBM(mesons.shape, jnp.float32)],
         scratch_shapes=[pltpu.SemaphoreType.DMA],

time: 65 us -> 64 us (0.985)
  Pallas kernels: 8.92 us -> 7.57 us
    pallas_call x2, Pallas kernels: 3.3 us -> 1.96 us  [the longest x1 1.12 us: partial_fields(): pl.pallas_call(own_kernel, in_specs=[vmem] * 4, out_specs=vmem, out_shape...]
  transfers between devices with their start and end apart: 2 -> 2, of which waited for: 1 -> 2; matrix products, arithmetic and copies ran while one was open for 0% -> 0% of each run, Pallas kernels for 3% -> 2%
where the time goes in v7:
time: 64 us; the launch traced here: 63.8 us
  blocking collectives  46.9 us (73%)
  Pallas kernels  7.57 us (12%)
  starting transfers between devices  7.37 us (12%)
  waiting for transfers between devices  1.14 us (2%)
  between operations  0.67 us (1%)
    all_to_all x3, blocking collectives, exchange(): return lax.all_to_all(array, axis, split_axis=0, concat_axis=0, tiled=True)  46.9 us
    pallas_call x1, Pallas kernels, partial_fields(): pl.pallas_call(field_kernel, in_specs=[hbm] * 4, out_specs=[vmem] * 4, ou...  4.77 us
    ppermute x1, starting transfers between devices, local(): traces = traces + lax.ppermute(traces, 'core', [(0, 1), (1, 0)])  4.08 us
    ppermute x1, starting transfers between devices, local(): arrived = lax.ppermute(peer, 'core', [(0, 1), (1, 0)])  3.29 us
  transfers between devices with their start and end apart: 2, of which 2 were waited for; matrix products, arithmetic and copies ran while one was open for 0% of the time, Pallas kernels for 2%

profile of v7, /device:TPU:1, one launch (start us, length us, event | category | flops | bytes accessed | tf_op | source)
XLA Modules:
  0.0 63.8 jit_solution(4244611472614738515)
XLA Ops:
  0.6 0.0 copy-start
  0.6 4.8 %fields.1 = (f32[896,128]{1,0:T(8,128)S(1)}, f32[27,8,128]{2,1,0:T(8,128)S(1)}, f32[27,8,128]{2,1,0:T(8,128)S(1)}, f32[8,5,32,256]{3,2,1,0:T(8,128)S(1)}) custom-call(s32[3,27]{1,0:T(4,128)} %bitcast.7, f32[16,128]{1,0:T(8,128)} %constant.2.clone.table_hbm, s32[12,64,512]{2,1,0:T(8,128)} %bitcast.11, bf16[12,512,128]{2,1,0:T(8,128)(2,1)} %bitcast.12), custom_call_target="tpu_custom_call" | custom-call | tf_op jit(solution)/shard_map/fields/pallas_call | solution.py:201
  5.4 3.3 %collective-permute-start = (f32[896,128]{1,0:T(8,128)S(1)}, f32[896,128]{1,0:T(8,128)S(1)}, u32[]{:S(2)}, u32[]{:S(2)}) collective-permute-start(f32[896,128]{1,0:T(8,128)S(1)} %get-tuple-element.13), channel_id=1, source_target_pairs={{0,8},{8,0},{1,9},{9,1},{2,10},{10,2},{3,11},{11,3},{4,12},{12,4},... | collective-permute-start | bytes 1376264 | tf_op jit(solution)/shard_map/ppermute | solution.py:323
  8.7 0.0 copy-done
  8.7 1.1 %own.1 = f32[896,128]{1,0:T(8,128)S(1)} custom-call(s32[3,27]{1,0:T(4,128)S(1)} %bitcast.8, f32[27,8,128]{2,1,0:T(8,128)S(1)} %get-tuple-element.10.phase_re, f32[27,8,128]{2,1,0:T(8,128)S(1)} %get-tuple-element.11.phase_im, f32[8,5,32,256]{3,2,1,0:T(8,128)S(1)} %get-tuple-element.12.d_ref), custom_call_target="tpu_custom_call" | custom-call | tf_op jit(solution)/shard_map/own/pallas_call | solution.py:219
  9.8 0.0 copy-start.1
  9.8 0.3 collective-permute-done
  10.2 0.1 add.6
  10.2 25.2 %all_to_all.15.part_ref = f32[16,56,128]{2,1,0:T(8,128)S(1)} all-to-all(f32[16,56,128]{2,1,0:T(8,128)S(1)} %bitcast.10), channel_id=1, replica_groups=mesh['z'=8,'yh'=2,'core'=2,'tm'=8] {'z','yh'}, dimensions={0} | all-to-all | bytes 917504 | tf_op jit(solution)/shard_map/all_to_all | solution.py:316
  35.4 0.2 mesons.1
  35.6 9.6 %all_to_all.16.fields_ref = f32[8,56,128]{2,1,0:T(8,128)S(1)} all-to-all(f32[8,56,128]{2,1,0:T(8,128)S(1)} %get-tuple-element.15), channel_id=1, replica_groups=mesh['z'=8,'yh'=2,'core'=2,'tm'=8] {'tm'}, dimensions={0} | all-to-all | bytes 458752 | tf_op jit(solution)/shard_map/all_to_all | solution.py:316
  45.2 0.0 copy-done.1
  45.2 0.8 %traces.1 = (f32[4,128]{1,0:T(4,128)S(1)}, f32[1,2,27,2,64]{4,3,2,1,0:T(2,128)}) custom-call(s32[2,8]{1,0:T(2,128)S(1)} %bitcast.9, f32[1,2,27,2,64]{4,3,2,1,0:T(2,128)S(1)} %get-tuple-element.14.mesons_ref, f32[8,56,128]{2,1,0:T(8,128)S(1)} %all_to_all.16.fields_ref), custom_call_target="tpu_custom_call" | custom-call | tf_op jit(solution)/shard_map/traces/pallas_call | solution.py:282
  46.0 4.1 %collective-permute-start.1 = (f32[4,128]{1,0:T(4,128)S(1)}, f32[4,128]{1,0:T(4,128)S(1)}, u32[]{:S(2)}, u32[]{:S(2)}) collective-permute-start(f32[4,128]{1,0:T(4,128)S(1)} %get-tuple-element.17), channel_id=1, source_target_pairs={{0,8},{8,0},{1,9},{9,1},{2,10},{10,2},{3,11},{11,3},{4,12},{12,4},... | collective-permute-start | bytes 6152 | tf_op jit(solution)/shard_map/ppermute | solution.py:327
  50.1 0.8 %collective-permute-done.1 = f32[4,128]{1,0:T(4,128)S(1)} collective-permute-done((f32[4,128]{1,0:T(4,128)S(1)}, f32[4,128]{1,0:T(4,128)S(1)}, u32[]{:S(2)}, u32[]{:S(2)}) %collective-permute-start.1) | collective-permute-done | bytes 2080 | tf_op jit(solution)/shard_map/ppermute | solution.py:327
  50.9 12.2 %all_to_all.17.part_ref = f32[16,4,128]{2,1,0:T(4,128)S(1)} all-to-all(f32[16,4,128]{2,1,0:T(4,128)S(1)} %broadcast_in_dim.3), channel_id=1, replica_groups=mesh['z'=8,'yh'=2,'core'=2,'tm'=8] {'z','yh'}, dimensions={0} | all-to-all | bytes 65536 | tf_op jit(solution)/shard_map/all_to_all | solution.py:316
  63.1 0.7 %correlators.1 = f32[8,2,27]{2,1,0:T(2,128)} custom-call(f32[16,4,128]{2,1,0:T(4,128)S(1)} %all_to_all.17.part_ref), custom_call_target="tpu_custom_call" | custom-call | tf_op jit(solution)/shard_map/correlators/pallas_call | solution.py:307
  (2 shorter events, 0.0 us)
Async XLA Ops:
  0.6 8.1 %copy-start = (s32[27,3]{0,1:T(4,128)S(1)}, s32[27,3]{0,1:T(4,128)}, u32[]{:S(2)}) copy-start(s32[27,3]{0,1:T(4,128)} %param.7) | copy-start | bytes 976
  5.4 4.7 %collective-permute-start = (f32[896,128]{1,0:T(8,128)S(1)}, f32[896,128]{1,0:T(8,128)S(1)}, u32[]{:S(2)}, u32[]{:S(2)}) collective-permute-start(f32[896,128]{1,0:T(8,128)S(1)} %get-tuple-element.13), channel_id=1, source_target_pairs={{0,8},{8,0},{1,9},{9,1},{2,10},{10,2},{3,11},{11,3},{4,12},{12,4},... | collective-permute-start | bytes 1376264 | tf_op jit(solution)/shard_map/ppermute | solution.py:323
  9.8 35.3 %copy-start.1 = (s32[8,2]{0,1:T(2,128)S(1)}, s32[8,2]{0,1:T(2,128)}, u32[]{:S(2)}) copy-start(s32[8,2]{0,1:T(2,128)} %param.8) | copy-start | bytes 196
  46.0 4.9 %collective-permute-start.1 = (f32[4,128]{1,0:T(4,128)S(1)}, f32[4,128]{1,0:T(4,128)S(1)}, u32[]{:S(2)}, u32[]{:S(2)}) collective-permute-start(f32[4,128]{1,0:T(4,128)S(1)} %get-tuple-element.17), channel_id=1, source_target_pairs={{0,8},{8,0},{1,9},{9,1},{2,10},{10,2},{3,11},{11,3},{4,12},{12,4},... | collective-permute-start | bytes 6152 | tf_op jit(solution)/shard_map/ppermute | solution.py:327

commit v8 on v7

--- a/solution.py
+++ b/solution.py
@@ -147,11 +147,11 @@
             for a in (2 * pair, 2 * pair + 1):
                 firsts = [c * 2 + b for c in (1 - core, core) for b in range(2)]
                 parts = [noise_ref[step, a, pl.ds(first, ZY, stride=4), :] for first in firsts]
-                rows.append(jnp.concatenate(parts, axis=0))
+                rows.append(jnp.concatenate(parts, axis=0).astype(jnp.float32).astype(jnp.bfloat16))
             turned = [pltpu.roll(r, SITE_BLOCK, 1) for r in rows]
             halves = (jnp.where(low64, rows[0], turned[1]), jnp.where(low64, turned[0], rows[1]))
             for g in range(2):
-                turns = halves[g].astype(jnp.float32).astype(jnp.bfloat16)
+                turns = halves[g]
                 er = jnp.abs(turns - two) - one
                 ei = jnp.abs(turns - one) - one
                 left_re, left_im = ([er], [ei])

time: 64 us -> 63.9 us (level)
  no operation moved by 1% of the time
where the time goes in v8:
time: 63.9 us; the launch traced here: 63.7 us
  blocking collectives  46.9 us (73%)
  Pallas kernels  7.54 us (12%)
  starting transfers between devices  7.37 us (12%)
  waiting for transfers between devices  1.14 us (2%)
  between operations  0.67 us (1%)
    all_to_all x3, blocking collectives, exchange(): return lax.all_to_all(array, axis, split_axis=0, concat_axis=0, tiled=True)  46.9 us
    pallas_call x1, Pallas kernels, partial_fields(): pl.pallas_call(field_kernel, in_specs=[hbm] * 4, out_specs=[vmem] * 4, ou...  4.74 us
    ppermute x1, starting transfers between devices, local(): traces = traces + lax.ppermute(traces, 'core', [(0, 1), (1, 0)])  4.08 us
    ppermute x1, starting transfers between devices, local(): arrived = lax.ppermute(peer, 'core', [(0, 1), (1, 0)])  3.29 us
  transfers between devices with their start and end apart: 2, of which 2 were waited for; matrix products, arithmetic and copies ran while one was open for 0% of the time, Pallas kernels for 2%

profile of v8, /device:TPU:1, one launch (start us, length us, event | category | flops | bytes accessed | tf_op | source)
XLA Modules:
  0.0 63.7 jit_solution(434662912254019309)
XLA Ops:
  0.6 0.0 copy-start
  0.6 4.7 %fields.1 = (f32[896,128]{1,0:T(8,128)S(1)}, f32[27,8,128]{2,1,0:T(8,128)S(1)}, f32[27,8,128]{2,1,0:T(8,128)S(1)}, f32[8,5,32,256]{3,2,1,0:T(8,128)S(1)}) custom-call(s32[3,27]{1,0:T(4,128)} %bitcast.7, f32[16,128]{1,0:T(8,128)} %constant.2.clone.table_hbm, s32[12,64,512]{2,1,0:T(8,128)} %bitcast.11, bf16[12,512,128]{2,1,0:T(8,128)(2,1)} %bitcast.12), custom_call_target="tpu_custom_call" | custom-call | tf_op jit(solution)/shard_map/fields/pallas_call | solution.py:201
  5.4 3.3 %collective-permute-start = (f32[896,128]{1,0:T(8,128)S(1)}, f32[896,128]{1,0:T(8,128)S(1)}, u32[]{:S(2)}, u32[]{:S(2)}) collective-permute-start(f32[896,128]{1,0:T(8,128)S(1)} %get-tuple-element.13), channel_id=1, source_target_pairs={{0,8},{8,0},{1,9},{9,1},{2,10},{10,2},{3,11},{11,3},{4,12},{12,4},... | collective-permute-start | bytes 1376264 | tf_op jit(solution)/shard_map/ppermute | solution.py:323
  8.7 0.0 copy-done
  8.7 1.1 %own.1 = f32[896,128]{1,0:T(8,128)S(1)} custom-call(s32[3,27]{1,0:T(4,128)S(1)} %bitcast.8, f32[27,8,128]{2,1,0:T(8,128)S(1)} %get-tuple-element.10.phase_re, f32[27,8,128]{2,1,0:T(8,128)S(1)} %get-tuple-element.11.phase_im, f32[8,5,32,256]{3,2,1,0:T(8,128)S(1)} %get-tuple-element.12.d_ref), custom_call_target="tpu_custom_call" | custom-call | tf_op jit(solution)/shard_map/own/pallas_call | solution.py:219
  9.8 0.0 copy-start.1
  9.8 0.3 collective-permute-done
  10.1 0.1 add.6
  10.2 25.2 %all_to_all.15.part_ref = f32[16,56,128]{2,1,0:T(8,128)S(1)} all-to-all(f32[16,56,128]{2,1,0:T(8,128)S(1)} %bitcast.10), channel_id=1, replica_groups=mesh['z'=8,'yh'=2,'core'=2,'tm'=8] {'z','yh'}, dimensions={0} | all-to-all | bytes 917504 | tf_op jit(solution)/shard_map/all_to_all | solution.py:316
  35.4 0.2 mesons.1
  35.5 9.6 %all_to_all.16.fields_ref = f32[8,56,128]{2,1,0:T(8,128)S(1)} all-to-all(f32[8,56,128]{2,1,0:T(8,128)S(1)} %get-tuple-element.15), channel_id=1, replica_groups=mesh['z'=8,'yh'=2,'core'=2,'tm'=8] {'tm'}, dimensions={0} | all-to-all | bytes 458752 | tf_op jit(solution)/shard_map/all_to_all | solution.py:316
  45.1 0.0 copy-done.1
  45.1 0.8 %traces.1 = (f32[4,128]{1,0:T(4,128)S(1)}, f32[1,2,27,2,64]{4,3,2,1,0:T(2,128)}) custom-call(s32[2,8]{1,0:T(2,128)S(1)} %bitcast.9, f32[1,2,27,2,64]{4,3,2,1,0:T(2,128)S(1)} %get-tuple-element.14.mesons_ref, f32[8,56,128]{2,1,0:T(8,128)S(1)} %all_to_all.16.fields_ref), custom_call_target="tpu_custom_call" | custom-call | tf_op jit(solution)/shard_map/traces/pallas_call | solution.py:282
  46.0 4.1 %collective-permute-start.1 = (f32[4,128]{1,0:T(4,128)S(1)}, f32[4,128]{1,0:T(4,128)S(1)}, u32[]{:S(2)}, u32[]{:S(2)}) collective-permute-start(f32[4,128]{1,0:T(4,128)S(1)} %get-tuple-element.17), channel_id=1, source_target_pairs={{0,8},{8,0},{1,9},{9,1},{2,10},{10,2},{3,11},{11,3},{4,12},{12,4},... | collective-permute-start | bytes 6152 | tf_op jit(solution)/shard_map/ppermute | solution.py:327
  50.1 0.8 %collective-permute-done.1 = f32[4,128]{1,0:T(4,128)S(1)} collective-permute-done((f32[4,128]{1,0:T(4,128)S(1)}, f32[4,128]{1,0:T(4,128)S(1)}, u32[]{:S(2)}, u32[]{:S(2)}) %collective-permute-start.1) | collective-permute-done | bytes 2080 | tf_op jit(solution)/shard_map/ppermute | solution.py:327
  50.9 12.2 %all_to_all.17.part_ref = f32[16,4,128]{2,1,0:T(4,128)S(1)} all-to-all(f32[16,4,128]{2,1,0:T(4,128)S(1)} %broadcast_in_dim.3), channel_id=1, replica_groups=mesh['z'=8,'yh'=2,'core'=2,'tm'=8] {'z','yh'}, dimensions={0} | all-to-all | bytes 65536 | tf_op jit(solution)/shard_map/all_to_all | solution.py:316
  63.0 0.7 %correlators.1 = f32[8,2,27]{2,1,0:T(2,128)} custom-call(f32[16,4,128]{2,1,0:T(4,128)S(1)} %all_to_all.17.part_ref), custom_call_target="tpu_custom_call" | custom-call | tf_op jit(solution)/shard_map/correlators/pallas_call | solution.py:307
  (2 shorter events, 0.0 us)
Async XLA Ops:
  0.6 8.1 %copy-start = (s32[27,3]{0,1:T(4,128)S(1)}, s32[27,3]{0,1:T(4,128)}, u32[]{:S(2)}) copy-start(s32[27,3]{0,1:T(4,128)} %param.7) | copy-start | bytes 976
  5.4 4.7 %collective-permute-start = (f32[896,128]{1,0:T(8,128)S(1)}, f32[896,128]{1,0:T(8,128)S(1)}, u32[]{:S(2)}, u32[]{:S(2)}) collective-permute-start(f32[896,128]{1,0:T(8,128)S(1)} %get-tuple-element.13), channel_id=1, source_target_pairs={{0,8},{8,0},{1,9},{9,1},{2,10},{10,2},{3,11},{11,3},{4,12},{12,4},... | collective-permute-start | bytes 1376264 | tf_op jit(solution)/shard_map/ppermute | solution.py:323
  9.8 35.3 %copy-start.1 = (s32[8,2]{0,1:T(2,128)S(1)}, s32[8,2]{0,1:T(2,128)}, u32[]{:S(2)}) copy-start(s32[8,2]{0,1:T(2,128)} %param.8) | copy-start | bytes 196
  46.0 4.9 %collective-permute-start.1 = (f32[4,128]{1,0:T(4,128)S(1)}, f32[4,128]{1,0:T(4,128)S(1)}, u32[]{:S(2)}, u32[]{:S(2)}) collective-permute-start(f32[4,128]{1,0:T(4,128)S(1)} %get-tuple-element.17), channel_id=1, source_target_pairs={{0,8},{8,0},{1,9},{9,1},{2,10},{10,2},{3,11},{11,3},{4,12},{12,4},... | collective-permute-start | bytes 6152 | tf_op jit(solution)/shard_map/ppermute | solution.py:327

commit v9 on v8

--- a/solution.py
+++ b/solution.py
@@ -326,7 +326,7 @@
     traces, mesons = partial_traces(pairs.T, mesons, exchange(copies, "tm"))
     traces = traces + lax.ppermute(traces, "core", [(0, 1), (1, 0)])
     spread = jnp.broadcast_to(traces, (ZY, *traces.shape))
-    correlators = summed_traces(exchange(spread, ("z", "yh")), 1.0 / 64, pairs.shape[0], nmom)
+    correlators = summed_traces(exchange(spread, ("yh", "z")), 1.0 / 64, pairs.shape[0], nmom)
     return (mesons, correlators)
 
 

time: 63.9 us -> 63.6 us (level)
  no operation moved by 1% of the time
where the time goes in v9:
time: 63.6 us; the launch traced here: 63.4 us
  blocking collectives  46.6 us (73%)
  Pallas kernels  7.54 us (12%)
  starting transfers between devices  7.37 us (12%)
  waiting for transfers between devices  1.14 us (2%)
  between operations  0.67 us (1%)
    all_to_all x3, blocking collectives, exchange(): return lax.all_to_all(array, axis, split_axis=0, concat_axis=0, tiled=True)  46.6 us
    pallas_call x1, Pallas kernels, partial_fields(): pl.pallas_call(field_kernel, in_specs=[hbm] * 4, out_specs=[vmem] * 4, ou...  4.74 us
    ppermute x1, starting transfers between devices, local(): traces = traces + lax.ppermute(traces, 'core', [(0, 1), (1, 0)])  4.08 us
    ppermute x1, starting transfers between devices, local(): arrived = lax.ppermute(peer, 'core', [(0, 1), (1, 0)])  3.29 us
  transfers between devices with their start and end apart: 2, of which 2 were waited for; matrix products, arithmetic and copies ran while one was open for 0% of the time, Pallas kernels for 2%

profile of v9, /device:TPU:1, one launch (start us, length us, event | category | flops | bytes accessed | tf_op | source)
XLA Modules:
  0.0 63.4 jit_solution(14362830501878633936)
XLA Ops:
  0.6 0.0 copy-start
  0.6 4.7 %fields.1 = (f32[896,128]{1,0:T(8,128)S(1)}, f32[27,8,128]{2,1,0:T(8,128)S(1)}, f32[27,8,128]{2,1,0:T(8,128)S(1)}, f32[8,5,32,256]{3,2,1,0:T(8,128)S(1)}) custom-call(s32[3,27]{1,0:T(4,128)} %bitcast.7, f32[16,128]{1,0:T(8,128)} %constant.2.clone.table_hbm, s32[12,64,512]{2,1,0:T(8,128)} %bitcast.11, bf16[12,512,128]{2,1,0:T(8,128)(2,1)} %bitcast.12), custom_call_target="tpu_custom_call" | custom-call | tf_op jit(solution)/shard_map/fields/pallas_call | solution.py:201
  5.4 3.3 %collective-permute-start = (f32[896,128]{1,0:T(8,128)S(1)}, f32[896,128]{1,0:T(8,128)S(1)}, u32[]{:S(2)}, u32[]{:S(2)}) collective-permute-start(f32[896,128]{1,0:T(8,128)S(1)} %get-tuple-element.13), channel_id=1, source_target_pairs={{0,8},{8,0},{1,9},{9,1},{2,10},{10,2},{3,11},{11,3},{4,12},{12,4},... | collective-permute-start | bytes 1376264 | tf_op jit(solution)/shard_map/ppermute | solution.py:323
  8.7 0.0 copy-done
  8.7 1.1 %own.1 = f32[896,128]{1,0:T(8,128)S(1)} custom-call(s32[3,27]{1,0:T(4,128)S(1)} %bitcast.8, f32[27,8,128]{2,1,0:T(8,128)S(1)} %get-tuple-element.10.phase_re, f32[27,8,128]{2,1,0:T(8,128)S(1)} %get-tuple-element.11.phase_im, f32[8,5,32,256]{3,2,1,0:T(8,128)S(1)} %get-tuple-element.12.d_ref), custom_call_target="tpu_custom_call" | custom-call | tf_op jit(solution)/shard_map/own/pallas_call | solution.py:219
  9.8 0.0 copy-start.1
  9.8 0.3 collective-permute-done
  10.1 0.1 add.6
  10.2 25.2 %all_to_all.15.part_ref = f32[16,56,128]{2,1,0:T(8,128)S(1)} all-to-all(f32[16,56,128]{2,1,0:T(8,128)S(1)} %bitcast.10), channel_id=1, replica_groups=mesh['z'=8,'yh'=2,'core'=2,'tm'=8] {'z','yh'}, dimensions={0} | all-to-all | bytes 917504 | tf_op jit(solution)/shard_map/all_to_all | solution.py:316
  35.4 0.2 mesons.1
  35.5 9.6 %all_to_all.16.fields_ref = f32[8,56,128]{2,1,0:T(8,128)S(1)} all-to-all(f32[8,56,128]{2,1,0:T(8,128)S(1)} %get-tuple-element.15), channel_id=1, replica_groups=mesh['z'=8,'yh'=2,'core'=2,'tm'=8] {'tm'}, dimensions={0} | all-to-all | bytes 458752 | tf_op jit(solution)/shard_map/all_to_all | solution.py:316
  45.1 0.0 copy-done.1
  45.1 0.8 %traces.1 = (f32[4,128]{1,0:T(4,128)S(1)}, f32[1,2,27,2,64]{4,3,2,1,0:T(2,128)}) custom-call(s32[2,8]{1,0:T(2,128)S(1)} %bitcast.9, f32[1,2,27,2,64]{4,3,2,1,0:T(2,128)S(1)} %get-tuple-element.14.mesons_ref, f32[8,56,128]{2,1,0:T(8,128)S(1)} %all_to_all.16.fields_ref), custom_call_target="tpu_custom_call" | custom-call | tf_op jit(solution)/shard_map/traces/pallas_call | solution.py:282
  46.0 4.1 %collective-permute-start.1 = (f32[4,128]{1,0:T(4,128)S(1)}, f32[4,128]{1,0:T(4,128)S(1)}, u32[]{:S(2)}, u32[]{:S(2)}) collective-permute-start(f32[4,128]{1,0:T(4,128)S(1)} %get-tuple-element.17), channel_id=1, source_target_pairs={{0,8},{8,0},{1,9},{9,1},{2,10},{10,2},{3,11},{11,3},{4,12},{12,4},... | collective-permute-start | bytes 6152 | tf_op jit(solution)/shard_map/ppermute | solution.py:327
  50.1 0.8 %collective-permute-done.1 = f32[4,128]{1,0:T(4,128)S(1)} collective-permute-done((f32[4,128]{1,0:T(4,128)S(1)}, f32[4,128]{1,0:T(4,128)S(1)}, u32[]{:S(2)}, u32[]{:S(2)}) %collective-permute-start.1) | collective-permute-done | bytes 2080 | tf_op jit(solution)/shard_map/ppermute | solution.py:327
  50.9 11.8 %all_to_all.17.part_ref = f32[16,4,128]{2,1,0:T(4,128)S(1)} all-to-all(f32[16,4,128]{2,1,0:T(4,128)S(1)} %broadcast_in_dim.3), channel_id=1, replica_groups=mesh['z'=8,'yh'=2,'core'=2,'tm'=8] {'yh','z'}, dimensions={0} | all-to-all | bytes 65536 | tf_op jit(solution)/shard_map/all_to_all | solution.py:316
  62.7 0.7 %correlators.1 = f32[8,2,27]{2,1,0:T(2,128)} custom-call(f32[16,4,128]{2,1,0:T(4,128)S(1)} %all_to_all.17.part_ref), custom_call_target="tpu_custom_call" | custom-call | tf_op jit(solution)/shard_map/correlators/pallas_call | solution.py:307
  (2 shorter events, 0.0 us)
Async XLA Ops:
  0.6 8.1 %copy-start = (s32[27,3]{0,1:T(4,128)S(1)}, s32[27,3]{0,1:T(4,128)}, u32[]{:S(2)}) copy-start(s32[27,3]{0,1:T(4,128)} %param.7) | copy-start | bytes 976
  5.4 4.7 %collective-permute-start = (f32[896,128]{1,0:T(8,128)S(1)}, f32[896,128]{1,0:T(8,128)S(1)}, u32[]{:S(2)}, u32[]{:S(2)}) collective-permute-start(f32[896,128]{1,0:T(8,128)S(1)} %get-tuple-element.13), channel_id=1, source_target_pairs={{0,8},{8,0},{1,9},{9,1},{2,10},{10,2},{3,11},{11,3},{4,12},{12,4},... | collective-permute-start | bytes 1376264 | tf_op jit(solution)/shard_map/ppermute | solution.py:323
  9.8 35.3 %copy-start.1 = (s32[8,2]{0,1:T(2,128)S(1)}, s32[8,2]{0,1:T(2,128)}, u32[]{:S(2)}) copy-start(s32[8,2]{0,1:T(2,128)} %param.8) | copy-start | bytes 196
  46.0 4.9 %collective-permute-start.1 = (f32[4,128]{1,0:T(4,128)S(1)}, f32[4,128]{1,0:T(4,128)S(1)}, u32[]{:S(2)}, u32[]{:S(2)}) collective-permute-start(f32[4,128]{1,0:T(4,128)S(1)} %get-tuple-element.17), channel_id=1, source_target_pairs={{0,8},{8,0},{1,9},{9,1},{2,10},{10,2},{3,11},{11,3},{4,12},{12,4},... | collective-permute-start | bytes 6152 | tf_op jit(solution)/shard_map/ppermute | solution.py:327
